TPU v7x, 128 devices: a whole 4x4x4 slice. The times are simulated.
128 devices in a mesh: wide: 32 (over y, z, core), narrow: 4 (over x).
Axes of the slice: x: 4, y: 4, z: 4, core: 2. Of those that a mesh axis runs over, the one named last changes fastest.
Arguments:
- object_field: float32 [2, 2048, 16384], P(None, 'narrow', 'wide')
- probe: float32 [4, 2, 256, 256], replicated, may hold values from -3 to 3
- patterns: float32 [4, 32, 6, 256, 256], P('narrow', 'wide'), may hold values from 0.1 to 4
- offsets: int32 [4, 32, 6, 2], P('narrow', 'wide'), may hold values from -128 to 384
- counts: int32 [4, 32], P('narrow', 'wide'), may hold values from 1 to 6
Outputs:
- object_new: float32 [2, 2048, 16384], P(None, 'narrow', 'wide')
- probe_new: float32 [4, 2, 256, 256], replicated
Inputs may be any that keep to these rules, and one draw needn't show every extreme that they name: A patch of 256 x 256 pixels at these offsets stays within the tile extended by 128 pixels on each side. `counts`: slots 0 to count - 1 of a tile are live, the others are ignored.
All inputs are finite; a program needn't handle non-finite values.
Results may differ from a plain program's by a relative error of at most 0.0003.
Values sent between devices are 32-bit elements; how exact they have to be, the bound alone decides.
A program may use at most 128 MiB of HBM per device.

v0:
```python
import jax
import jax.numpy as jnp
from jax import lax
from jax.sharding import PartitionSpec as P

H = 128
BATCHES = 3
POS = 2


def extended(shard, sides, width):
    for axis, dim in sides:
        size, length = (lax.axis_size(axis), shard.shape[dim])
        up = [(i, (i + 1) % size) for i in range(size - 1)]
        down = [(j, i) for i, j in up]
        last = lax.slice_in_dim(shard, length - width, length, axis=dim)
        leading = lax.slice_in_dim(shard, 0, width, axis=dim)
        before = lax.ppermute(last, axis, up)
        after = lax.ppermute(leading, axis, down)
        shard = jnp.concatenate([before, shard, after], axis=dim)
    return shard


def shifted(value, axis, steps):
    count = lax.axis_size(axis)
    leading, last = (max(0, -steps), min(count, count - steps))
    return lax.ppermute(value, axis, [(source, source + steps) for source in range(leading, last)])


def dft_tables(size):
    index = jnp.arange(size, dtype=jnp.int32)
    phase = index[:, None] * index[None, :] % size
    angle = -2.0 * jnp.pi * phase.astype(jnp.float32) / size
    scale = 1.0 / jnp.sqrt(jnp.float32(size))
    return (jnp.cos(angle) * scale, jnp.sin(angle) * scale)


def transform(real_part, imag_part, table_re, table_im):
    high = lax.Precision.HIGHEST
    left_re = jnp.einsum("jk,mkl->mjl", table_re, real_part, precision=high) - jnp.einsum(
        "jk,mkl->mjl", table_im, imag_part, precision=high
    )
    left_im = jnp.einsum("jk,mkl->mjl", table_re, imag_part, precision=high) + jnp.einsum(
        "jk,mkl->mjl", table_im, real_part, precision=high
    )
    out_re = jnp.einsum("mjk,kl->mjl", left_re, table_re, precision=high) - jnp.einsum(
        "mjk,kl->mjl", left_im, table_im, precision=high
    )
    out_im = jnp.einsum("mjk,kl->mjl", left_re, table_im, precision=high) + jnp.einsum(
        "mjk,kl->mjl", left_im, table_re, precision=high
    )
    return (out_re, out_im)


def slot_terms(patch, probe, measured, table_re, table_im):
    probe_re = probe[:, 0]
    probe_im = probe[:, 1]
    obj_re = patch[0]
    obj_im = patch[1]
    psi_re = probe_re * obj_re - probe_im * obj_im
    psi_im = probe_re * obj_im + probe_im * obj_re
    far_re, far_im = transform(psi_re, psi_im, table_re, table_im)
    intensity = jnp.sum(far_re * far_re + far_im * far_im, axis=0)
    keep = 1.0 - jnp.sqrt(measured) / jnp.sqrt(intensity + 0.1)
    back_re, back_im = transform(far_re * keep, far_im * keep, table_re, -table_im)
    grad_re = jnp.sum(probe_re * back_re + probe_im * back_im, axis=0)
    grad_im = jnp.sum(probe_re * back_im - probe_im * back_re, axis=0)
    pgrad_re = obj_re * back_re + obj_im * back_im
    pgrad_im = obj_re * back_im - obj_im * back_re
    square = jnp.sum(obj_re * obj_re + obj_im * obj_im)
    return (jnp.stack([grad_re, grad_im]), jnp.stack([pgrad_re, pgrad_im], axis=1), square)


def local(object_field, probe, patterns, offsets, counts):
    tile = object_field.shape[1]
    size = probe.shape[-1]
    table_re, table_im = dft_tables(size)
    padded = extended(object_field, (("wide", 2), ("narrow", 1)), H)
    gradient = jnp.zeros_like(padded)
    count_here = counts[0, 0]
    zero_at = jnp.zeros((), jnp.int32)
    for minibatch in range(BATCHES):
        probe_grad = jnp.zeros_like(probe)
        coverage = jnp.zeros((), jnp.float32)
        for position in range(POS):
            slot_at = minibatch * POS + position
            row_at = offsets[0, 0, slot_at, 0] + H
            col_at = offsets[0, 0, slot_at, 1] + H
            patch = lax.dynamic_slice(padded, (zero_at, row_at, col_at), (2, size, size))
            measured = patterns[0, 0, slot_at]

            def active(operands):
                return slot_terms(operands[0], operands[1], operands[2], table_re, table_im)

            def inactive(operands):
                return (
                    jnp.zeros((2, size, size), jnp.float32),
                    jnp.zeros_like(probe),
                    jnp.zeros((), jnp.float32),
                )

            obj_grad, pgrad, square = lax.cond(
                slot_at < count_here, active, inactive, (patch, probe, measured)
            )
            old = lax.dynamic_slice(gradient, (zero_at, row_at, col_at), (2, size, size))
            gradient = lax.dynamic_update_slice(gradient, old + obj_grad, (zero_at, row_at, col_at))
            probe_grad = probe_grad + pgrad
            coverage = coverage + square
        summed, total_cover = lax.psum((probe_grad, coverage), ("wide", "narrow"))
        probe = probe - summed / (total_cover / (size * size))
    left_part = gradient[:, :, :H]
    right_part = gradient[:, :, tile + H :]
    from_right = shifted(left_part, "wide", -1)
    from_left = shifted(right_part, "wide", 1)
    gradient = gradient.at[:, :, tile : tile + H].add(from_right)
    gradient = gradient.at[:, :, H : 2 * H].add(from_left)
    upper_part = gradient[:, :H, H : tile + H]
    lower_part = gradient[:, tile + H :, H : tile + H]
    from_below = shifted(upper_part, "narrow", -1)
    from_above = shifted(lower_part, "narrow", 1)
    core = gradient[:, H : tile + H, H : tile + H]
    core = core.at[:, tile - H :, :].add(from_below)
    core = core.at[:, :H, :].add(from_above)
    power = jnp.sum(probe[:, 0] ** 2 + probe[:, 1] ** 2, axis=0)
    top = jnp.max(power)
    return (object_field - 0.5 * core / top, probe)


def solution(mesh):
    placed = (
        P(None, "narrow", "wide"),
        P(),
        P("narrow", "wide", None, None, None),
        P("narrow", "wide", None, None),
        P("narrow", "wide"),
    )
    return jax.shard_map(
        local,
        mesh=mesh,
        in_specs=placed,
        out_specs=(P(None, "narrow", "wide"), P()),
        check_vma=False,
    )
```

profile of v0, /device:TPU:1, one launch (start us, length us, event | category | flops | bytes accessed | tf_op | source)
XLA Modules:
  0.0 803.4 jit_solution(2545430750540542145)
XLA Ops:
  8.6 4.9 collective-permute-start
  13.6 1.9 collective-permute-start.1
  15.5 4.2 collective-permute-done
  19.9 4.2 collective-permute-done.1
  27.1 3.2 collective-permute-start.2
  38.9 2.7 collective-permute-done.2
  41.6 4.1 collective-permute-done.3
  45.7 4.6 pad_maximum_fusion.12
  50.3 37.3 %conditional.6 = (f32[2,256,256]{2,1,0:T(8,128)S(1)}, f32[]{:T(128)}, f32[4,2,256,256]{3,2,1,0:T(8,128)}) conditional(s32[]{:T(128)} %bitcast.174, () %tuple.80, (f32[4,2,256,256]{3,2,1,0:T(8,128)S(1)}, f32[2,768,768]{2,1,0:T(8,128)}, f32[256,256]{1,0:T(8,128)S(1)}, f32[256,256]{1,0:T(8,128)S(1)}, f32[256,256]{1,0:T(8,128)S(1)}, ...), branch_computations={%region_0.1_spmd, %region_1.6_spmd.clone} | conditional | flops 12897091584 | bytes 71303224 | solution.py:102
  50.5 2.0 add_reduce_fusion.14
  59.9 1.9 fusion.189
  61.8 1.9 fusion.196
  63.6 2.1 convolution_subtract_fusion.18
  65.7 2.0 add_reduce_fusion.13
  77.9 2.2 fusion.184
  80.1 1.9 convolution_add_fusion.16
  82.0 2.4 add_bitcast_fusion.4
  87.6 18.4 %conditional.7 = (f32[2,256,256]{2,1,0:T(8,128)S(1)}, f32[]{:T(128)}, f32[4,2,256,256]{3,2,1,0:T(8,128)}) conditional(s32[]{:T(128)} %bitcast.183, () %tuple.82, (f32[4,2,256,256]{3,2,1,0:T(8,128)S(1)}, f32[2,768,768]{2,1,0:T(8,128)}, f32[256,256]{1,0:T(8,128)S(1)}, f32[256,256]{1,0:T(8,128)S(1)}, f32[256,256]{1,0:T(8,128)S(1)}, ...), branch_computations={%region_6.7_spmd, %region_7.12_spmd.clone} | conditional | flops 12897091584 | bytes 71303224 | solution.py:102
  106.0 4.0 add.745
  115.3 91.4 %psum.43 = f32[]{:T(128)} all-reduce(f32[]{:T(128)S(6)} %add.746), channel_id=1, replica_groups=mesh['wide'=32,'narrow'=4] {'wide','narrow'}, use_global_device_ids=true, to_apply=%region_13.14 | all-reduce | flops 1 | bytes 8 | tf_op jit(solution)/shard_map/psum | solution.py:109
  207.4 80.2 %all-reduce.4.cloned.1.call-done = f32[4,2,256,256]{3,2,1,0:T(8,128)} async-done(((f32[4,2,256,256]{3,2,1,0:T(8,128)}), f32[4,2,256,256]{3,2,1,0:T(8,128)}) %all-reduce.4.cloned.1.call-update) | async-done | bytes 2097168 | tf_op jit(solution)/shard_map/psum | solution.py:109
  287.6 2.6 divide_subtract_fusion.3
  290.2 11.2 %conditional.8 = (f32[2,256,256]{2,1,0:T(8,128)}, f32[]{:T(128)}, f32[4,2,256,256]{3,2,1,0:T(8,128)}) conditional(s32[]{:T(128)} %bitcast.188, () %tuple.84, (f32[4,2,256,256]{3,2,1,0:T(8,128)S(1)}, f32[2,768,768]{2,1,0:T(8,128)}, s32[]{:T(128)}, s32[]{:T(128)}, f32[256,256]{1,0:T(8,128)S(1)}, /*index=5*/f32[256,256]{1,0:T(8,128)S(1)}, ...), branch_computations={%region_14.15_spmd, %region_15.20_spmd} | conditional | flops 12897091584 | bytes 71303224 | solution.py:102
  301.4 12.6 %conditional.9 = (f32[2,256,256]{2,1,0:T(8,128)}, f32[]{:T(128)}, f32[4,2,256,256]{3,2,1,0:T(8,128)}) conditional(s32[]{:T(128)} %bitcast.193, () %tuple.86, (f32[4,2,256,256]{3,2,1,0:T(8,128)S(1)}, f32[2,768,768]{2,1,0:T(8,128)}, s32[]{:T(128)}, s32[]{:T(128)}, f32[256,256]{1,0:T(8,128)S(1)}, /*index=5*/f32[256,256]{1,0:T(8,128)S(1)}, ...), branch_computations={%region_20.21_spmd, %region_21.26_spmd} | conditional | flops 12897091584 | bytes 71303224 | solution.py:102
  314.0 3.8 add.765
  322.6 2.5 broadcast_in_dim.2
  325.1 6.5 dynamic_update_slice.18
  333.1 6.5 dynamic_update_slice.19
  339.7 115.0 %psum.45 = f32[]{:T(128)} all-reduce(f32[]{:T(128)S(6)} %add.766), channel_id=1, replica_groups=mesh['wide'=32,'narrow'=4] {'wide','narrow'}, use_global_device_ids=true, to_apply=%region_27.28 | all-reduce | flops 1 | bytes 8 | tf_op jit(solution)/shard_map/psum | solution.py:109
  456.9 5.8 dynamic_update_slice.20
  464.2 6.8 dynamic_update_slice.21
  471.0 47.3 %all-reduce.6.cloned.1.call-done = f32[4,2,256,256]{3,2,1,0:T(8,128)} async-done(((f32[4,2,256,256]{3,2,1,0:T(8,128)}), f32[4,2,256,256]{3,2,1,0:T(8,128)}) %all-reduce.6.cloned.1.call-update) | async-done | bytes 2097168 | tf_op jit(solution)/shard_map/psum | solution.py:109
  518.3 3.2 divide_subtract_fusion.2
  521.5 11.6 %conditional.10 = (f32[2,256,256]{2,1,0:T(8,128)}, f32[]{:T(128)}, f32[4,2,256,256]{3,2,1,0:T(8,128)}) conditional(s32[]{:T(128)} %bitcast.198, () %tuple.88, (f32[4,2,256,256]{3,2,1,0:T(8,128)}, f32[2,768,768]{2,1,0:T(8,128)}, s32[]{:T(128)}, s32[]{:T(128)}, f32[256,256]{1,0:T(8,128)S(1)}, /*index=5*/f32[256,256]{1,0:T(8,128)S(1)}, ...), branch_computations={%region_28.29_spmd, %region_29.34_spmd} | conditional | flops 12897091584 | bytes 79691856 | solution.py:102
  534.8 6.5 dynamic_update_slice.22
  541.4 5.4 conditional.11
  548.1 6.0 dynamic_update_slice.23
  555.3 62.5 %collective-permute-start.4 = (f32[2,768,128]{2,1,0:T(8,128)S(1)}, f32[2,768,128]{2,1,0:T(8,128)S(1)}, u32[]{:S(2)}, u32[]{:S(2)}) collective-permute-start(f32[2,768,128]{2,1,0:T(8,128)S(1)} %slice.336), channel_id=1, source_target_pairs={{4,0},{8,4},{12,8},{16,12},{20,16},{24,20},{28,24},{32,28},{36,32}... | collective-permute-start | bytes 2359304 | tf_op jit(solution)/shard_map/ppermute | solution.py:27
  617.9 1.9 collective-permute-done.4
  619.8 2.7 fusion.259
  622.5 1.9 collective-permute-start.5
  624.4 3.8 add.781
  628.3 73.8 %psum.47 = f32[]{:T(128)} all-reduce(f32[]{:T(128)S(6)} %add.782), channel_id=1, replica_groups=mesh['wide'=32,'narrow'=4] {'wide','narrow'}, use_global_device_ids=true, to_apply=%region_41.42 | all-reduce | flops 1 | bytes 8 | tf_op jit(solution)/shard_map/psum | solution.py:109
  702.8 2.2 fusion.248
  704.9 2.3 fusion.258
  707.2 3.3 collective-permute-start.7
  711.8 74.8 %all-reduce.8.cloned.1.call-done = f32[4,2,256,256]{3,2,1,0:T(8,128)} async-done(((f32[4,2,256,256]{3,2,1,0:T(8,128)}), f32[4,2,256,256]{3,2,1,0:T(8,128)}) %all-reduce.8.cloned.1.call-update) | async-done | bytes 2097168 | tf_op jit(solution)/shard_map/psum | solution.py:109
  794.3 2.4 divide_subtract_fusion
  (69 shorter events, 54.9 us)
Async XLA Ops:
  7.2 12.6 %copy-start.3 = (f32[2,512,512]{2,1,0:T(8,128)S(1)}, f32[2,512,512]{2,1,0:T(8,128)}, u32[]{:S(2)}) copy-start(f32[2,512,512]{2,1,0:T(8,128)} %param.25) | copy-start | bytes 6291460
  7.2 280.5 %all-reduce.4.cloned.1.call-start = ((), (), s32[]{:S(2)}) async-start(), calls=%async_computation | async-start | bytes 4194304 | tf_op jit(solution)/shard_map/psum | solution.py:109
  8.6 11.0 %collective-permute-start = (f32[2,512,128]{2,1,0:T(8,128)S(1)}, f32[2,512,128]{2,1,0:T(8,128)S(1)}, u32[]{:S(2)}, u32[]{:S(2)}) collective-permute-start(f32[2,512,128]{2,1,0:T(8,128)S(1)} %get-tuple-element.871), channel_id=1, source_target_pairs={{0,4},{4,8},{8,12},{12,16},{16,20},{20,24},{24,28},{28,32},{32,36}... | collective-permute-start | bytes 1572872 | tf_op jit(solution)/shard_map/ppermute | solution.py:18
  13.6 10.5 %collective-permute-start.1 = (f32[2,512,128]{2,1,0:T(8,128)S(1)}, f32[2,512,128]{2,1,0:T(8,128)S(1)}, u32[]{:S(2)}, u32[]{:S(2)}) collective-permute-start(f32[2,512,128]{2,1,0:T(8,128)S(1)} %get-tuple-element.870), channel_id=1, source_target_pairs={{4,0},{8,4},{12,8},{16,12},{20,16},{24,20},{28,24},{32,28},{36,32}... | collective-permute-start | bytes 1572872 | tf_op jit(solution)/shard_map/ppermute | solution.py:19
  19.9 11.6 %copy-start.8 = (s32[1,1,6,2]{2,3,1,0:T(2,128)S(1)}, s32[1,1,6,2]{2,3,1,0:T(2,128)}, u32[]{:S(2)}) copy-start(s32[1,1,6,2]{2,3,1,0:T(2,128)} %param.28) | copy-start | bytes 148
  24.1 1.7 copy-start.5
  27.1 14.5 %collective-permute-start.2 = (f32[2,128,768]{2,1,0:T(8,128)}, f32[2,128,768]{2,1,0:T(8,128)S(1)}, u32[]{:S(2)}, u32[]{:S(2)}) collective-permute-start(f32[2,128,768]{2,1,0:T(8,128)} %get-tuple-element.868), channel_id=1, source_target_pairs={{0,1},{1,2},{2,3},{4,5},{5,6},{6,7},{8,9},{9,10},{10,11},{12,13},{... | collective-permute-start | bytes 2359304 | tf_op jit(solution)/shard_map/ppermute | solution.py:18
  30.2 15.5 %collective-permute-start.3 = (f32[2,128,768]{2,1,0:T(8,128)}, f32[2,128,768]{2,1,0:T(8,128)}, u32[]{:S(2)}, u32[]{:S(2)}) collective-permute-start(f32[2,128,768]{2,1,0:T(8,128)} %get-tuple-element.869), channel_id=1, source_target_pairs={{1,0},{2,1},{3,2},{5,4},{6,5},{7,6},{9,8},{10,9},{11,10},{13,12},{... | collective-permute-start | bytes 2359304 | tf_op jit(solution)/shard_map/ppermute | solution.py:19
  38.9 11.4 %copy-start.2 = (f32[4,2,256,256]{3,2,1,0:T(8,128)S(1)}, f32[4,2,256,256]{3,2,1,0:T(8,128)}, u32[]{:S(2)}) copy-start(f32[4,2,256,256]{3,2,1,0:T(8,128)} %param.26) | copy-start | bytes 6291460
  106.0 4.0 copy-start.7
  110.0 408.3 %all-reduce.6.cloned.1.call-start = ((), (), s32[]{:S(2)}) async-start(), calls=%async_computation.1 | async-start | bytes 4194304 | tf_op jit(solution)/shard_map/psum | solution.py:109
  317.8 468.8 %all-reduce.8.cloned.1.call-start = ((), (), s32[]{:S(2)}) async-start(), calls=%async_computation.2 | async-start | bytes 4194304 | tf_op jit(solution)/shard_map/psum | solution.py:109
  533.1 8.2 %copy-start = (f32[4,2,256,256]{3,2,1,0:T(8,128)S(1)}, f32[4,2,256,256]{3,2,1,0:T(8,128)}, u32[]{:S(2)}) copy-start(f32[4,2,256,256]{3,2,1,0:T(8,128)} %divide_subtract_fusion.2) | copy-start | bytes 6291460
  555.3 64.4 %collective-permute-start.4 = (f32[2,768,128]{2,1,0:T(8,128)S(1)}, f32[2,768,128]{2,1,0:T(8,128)S(1)}, u32[]{:S(2)}, u32[]{:S(2)}) collective-permute-start(f32[2,768,128]{2,1,0:T(8,128)S(1)} %slice.336), channel_id=1, source_target_pairs={{4,0},{8,4},{12,8},{16,12},{20,16},{24,20},{28,24},{32,28},{36,32}... | collective-permute-start | bytes 2359304 | tf_op jit(solution)/shard_map/ppermute | solution.py:27
  622.5 80.2 %collective-permute-start.5 = (f32[2,768,128]{2,1,0:T(8,128)}, f32[2,768,128]{2,1,0:T(8,128)S(1)}, u32[]{:S(2)}, u32[]{:S(2)}) collective-permute-start(f32[2,768,128]{2,1,0:T(8,128)} %get-tuple-element.866), channel_id=1, source_target_pairs={{0,4},{4,8},{8,12},{12,16},{16,20},{20,24},{24,28},{28,32},{32,36}... | collective-permute-start | bytes 2359304 | tf_op jit(solution)/shard_map/ppermute | solution.py:27
  707.2 86.7 %collective-permute-start.7 = (f32[2,128,512]{2,1,0:T(8,128)}, f32[2,128,512]{2,1,0:T(8,128)S(1)}, u32[]{:S(2)}, u32[]{:S(2)}) collective-permute-start(f32[2,128,512]{2,1,0:T(8,128)} %get-tuple-element.864), channel_id=1, source_target_pairs={{0,1},{1,2},{2,3},{4,5},{5,6},{6,7},{8,9},{9,10},{10,11},{12,13},{... | collective-permute-start | bytes 1572872 | tf_op jit(solution)/shard_map/ppermute | solution.py:27
  710.5 81.9 %collective-permute-start.6 = (f32[2,128,512]{2,1,0:T(8,128)}, f32[2,128,512]{2,1,0:T(8,128)}, u32[]{:S(2)}, u32[]{:S(2)}) collective-permute-start(f32[2,128,512]{2,1,0:T(8,128)} %get-tuple-element.865), channel_id=1, source_target_pairs={{1,0},{2,1},{3,2},{5,4},{6,5},{7,6},{9,8},{10,9},{11,10},{13,12},{... | collective-permute-start | bytes 1572872 | tf_op jit(solution)/shard_map/ppermute | solution.py:27
  788.5 1.3 copy-start.6
  792.4 1.9 copy-start.4
Sparse Core Ops, SparseCore 0:
  110.2 177.4 all-reduce.3
  318.0 200.3 all-reduce.5
  628.4 158.1 all-reduce.7
where the time goes:
time: 810 us; the launch traced here: 803 us
  blocking collectives  280 us (35%)
  waiting for transfers between devices  219 us (27%)
  starting transfers between devices  80.5 us (10%)
  local copies, waits for them, and re-layouts  64.4 us (8%)
  loops' own time  50.9 us (6%)
  other arithmetic  45.3 us (6%)
  between operations  31.9 us (4%)
  matrix products  30.8 us (4%)
    psum x3, blocking collectives, local(): summed, total_cover = lax.psum((probe_grad, coverage), ('wide', 'narrow'))  280 us
    psum x3, waiting for transfers between devices, local(): summed, total_cover = lax.psum((probe_grad, coverage), ('wide', 'narrow'))  202 us
    ppermute x4, starting transfers between devices, shifted(): lax.ppermute(value, axis, [(source, source + steps) for source in range(l...  69.1 us
    another operation x6, loops' own time, local(): lax.cond(slot_at < count_here, active, inactive, (patch, probe, measured))  50.9 us
    dynamic_update_slice x6, local copies, waits for them, and re-layouts, local(): lax.dynamic_update_slice(gradient, old + obj_grad, (zero_at, row_at, col_...  38.2 us
  transfers between devices with their start and end apart: 11, of which 8 were waited for; matrix products, arithmetic and copies ran while one was open for 6% of the time, Pallas kernels for 0%

commit v1 on v0

v1 whole, which is shorter than its diff:
```python
import jax
import jax.numpy as jnp
import ml_dtypes
import numpy as np
from jax import lax
from jax.experimental import pallas as pl
from jax.experimental.pallas import tpu as pltpu
from jax.sharding import PartitionSpec as P

H = 128
TILE = 512
R = 256
HALF = R // 2
MODES = 4
BATCHES = 3
POS = 2
MESH = pl.DeviceIdType.MESH
F32 = jnp.float32
BF16 = jnp.bfloat16

PARTS = 3
CHUNKS = 16
ROWS = 24
ORDER = ((0, 1, 2), (1, 2, 0), (2, 0, 1))
STEPS = (1, 2, 3)


def tables():
    k = np.arange(R)
    angle = 2.0 * np.pi * ((np.arange(HALF)[:, None] * k[None, :]) % R) / R
    upper = np.cos(angle)
    lower = np.sin(angle)
    lower[0] = np.where(k % 2 == 0, 1.0, -1.0)
    packed = (np.concatenate([upper, lower]) / np.sqrt(R)).astype(np.float32)
    order = np.concatenate([np.arange(HALF), [HALF], R - np.arange(1, HALF)])
    select = np.zeros((R, R), np.float32)
    select[np.arange(R), order] = 1.0

    def pair(value):
        high = value.astype(ml_dtypes.bfloat16)
        low = (value - high.astype(np.float32)).astype(ml_dtypes.bfloat16)
        return [high, low]

    pick = select.astype(ml_dtypes.bfloat16)
    return np.stack(pair(packed) + pair(packed.T.copy()) + [pick, pick.T.copy()])


def split(value):
    high = value.astype(BF16)
    return high, (value - high.astype(F32)).astype(BF16)


def dot(a, b):
    return jnp.dot(a, b, preferred_element_type=F32)


def left_product(table, value):
    high, low = split(value)
    return dot(table[0], high) + dot(table[0], low) + dot(table[1], high)


def right_product(value, table):
    high, low = split(value)
    return dot(high, table[0]) + dot(low, table[0]) + dot(high, table[1])


def row_mask(shape):
    return lax.broadcasted_iota(jnp.int32, shape, 0) == 0


def rows_fixed(first, general):
    top = jnp.where(row_mask(first[:8].shape), first[:8], general[:8])
    return jnp.concatenate([top, general[8:]], axis=0)


def butterfly(zr, zi):
    ur, vr, ui, vi = zr[:HALF], zr[HALF:], zi[:HALF], zi[HALF:]
    plus = (rows_fixed(ur, ur + vi), rows_fixed(ui, ui - vr))
    minus = (rows_fixed(vr, ur - vi), rows_fixed(vi, ui + vr))
    first = lax.broadcasted_iota(jnp.int32, (HALF, HALF), 1) == 0
    out = []
    for re, im in (plus, minus):
        ur, vr, ui, vi = re[:, :HALF], re[:, HALF:], im[:, :HALF], im[:, HALF:]
        mr, mi = jnp.where(first, 0.0, vr), jnp.where(first, 0.0, vi)
        out.append(
            (
                (ur + mi, ui - mr),
                (jnp.where(first, vr, ur - vi), jnp.where(first, vi, ui + vr)),
            )
        )
    return out


def butterfly_transposed(quads):
    first = lax.broadcasted_iota(jnp.int32, (HALF, HALF), 1) == 0
    sides = []
    for (pr, pi), (qr, qi) in quads:
        ur = pr + jnp.where(first, 0.0, qr)
        ui = pi + jnp.where(first, 0.0, qi)
        vr = jnp.where(first, qr, qi - pi)
        vi = jnp.where(first, qi, pr - qr)
        sides.append((jnp.concatenate([ur, vr], axis=1), jnp.concatenate([ui, vi], axis=1)))
    (pr, pi), (qr, qi) = sides
    ur = rows_fixed(pr, pr + qr)
    ui = rows_fixed(pi, pi + qi)
    vr = rows_fixed(qr, qi - pi)
    vi = rows_fixed(qi, pr - qr)
    return jnp.concatenate([ur, vr, ui, vi], axis=0)


def read_plane(ref, plane):
    if plane == 3:
        value = ref[pl.ds(2 * CHUNKS, CHUNKS), pl.ds(0, 16), :]
        return value.reshape(R, R)
    start, stop = plane * R, (plane + 1) * R
    low, high = start // ROWS, -(-stop // ROWS)
    value = ref[pl.ds(low, high - low)].reshape((high - low) * ROWS, R)
    return value[start - low * ROWS : stop - low * ROWS]


def write_plane(ref, plane, value):
    if plane == 3:
        for chunk in range(CHUNKS):
            ref[2 * CHUNKS + chunk, pl.ds(0, 16), :] = value[16 * chunk : 16 * chunk + 16]
        return
    for tile in range(R // 8):
        row = plane * R + 8 * tile
        ref[row // ROWS, pl.ds(row % ROWS, 8), :] = value[8 * tile : 8 * tile + 8]


def whole_kernel(
    offs, cnt, obj, probe, patterns, tabs,
    obj_out, probe_out,
    pad, pbuf, gbuf, spat, patch, far, og, zbuf, grad, cover,
    acc0, acc1, recv0, recv1, recv2, cross, hside, hvert, hcorn,
    bsend, brecv, hsend, hrecv, gsend, grecv,
):
    wide = lax.axis_index("wide")
    x = lax.axis_index("narrow")
    n_wide = lax.axis_size("wide")
    n_narrow = lax.axis_size("narrow")
    core = wide % 2
    z = (wide // 2) % 4
    y = wide // 8
    place = (x, y, z)
    table = (tabs.at[0], tabs.at[1])
    table_t = (tabs.at[2], tabs.at[3])

    def device(at, c):
        return ((at[1] * 4 + at[2]) * 2 + c, at[0])

    def peer(dim, step):
        at = list(place)
        at[dim] = (at[dim] + step) % 4
        return device(at, core)

    sibling = device(place, 1 - core)

    ways = ((-1, 0), (1, 0), (0, -1), (0, 1), (-1, -1), (1, -1), (-1, 1), (1, 1))

    def there(way):
        dw, dn = way
        ok = wide >= 0
        if dw:
            ok = (wide > 0) if dw < 0 else (wide < n_wide - 1)
        if dn:
            ok_n = (x > 0) if dn < 0 else (x < n_narrow - 1)
            ok = jnp.logical_and(ok, ok_n) if dw else ok_n
        return ok

    def away(way):
        return (wide + way[0], x + way[1])

    def border(way):
        dw, dn = way
        lane = {-1: (0, 1), 0: (1, 4), 1: (5, 1)}[dw]
        row = {-1: (0, H), 0: (H, TILE), 1: (H + TILE, H)}[dn]
        return lane, row

    def edge(way):
        dw, dn = way
        lane = {-1: (0, 1), 0: (0, 4), 1: (3, 1)}[dw]
        row = {-1: (0, H), 0: (0, TILE), 1: (TILE - H, H)}[dn]
        return lane, row

    for at in range(2):
        for lane in (0, 5):
            pad[at, lane] = jnp.zeros((TILE + 2 * H, H), F32)
        for lane in range(1, 5):
            pad[at, lane, pl.ds(0, H), :] = jnp.zeros((H, H), F32)
            pad[at, lane, pl.ds(H + TILE, H), :] = jnp.zeros((H, H), F32)
    hside[...] = jnp.zeros_like(hside)
    hvert[...] = jnp.zeros_like(hvert)
    hcorn[...] = jnp.zeros_like(hcorn)

    barrier = pltpu.get_barrier_semaphore()
    pl.semaphore_signal(barrier, inc=1, device_id=sibling, device_id_type=MESH)
    for dim in range(3):
        for step in STEPS:
            pl.semaphore_signal(barrier, inc=1, device_id=peer(dim, step), device_id_type=MESH)
    total = 10
    for way in ways:
        total = total + there(way).astype(jnp.int32)

        @pl.when(there(way))
        def _():
            pl.semaphore_signal(barrier, inc=1, device_id=away(way), device_id_type=MESH)

    pl.semaphore_wait(barrier, total)

    def halo(way, slot, lane):
        (lane_to, _), (row_to, rows) = border((-way[0], -way[1]))
        (lane_from, _), (row_from, _) = edge(way)
        return pltpu.make_async_remote_copy(
            src_ref=obj.at[:, pl.ds(row_from, rows), pl.ds((lane_from + lane) * H, H)],
            dst_ref=pad.at[:, lane_to + lane, pl.ds(row_to, rows), :],
            send_sem=hsend.at[slot],
            recv_sem=hrecv.at[slot],
            device_id=away(way),
            device_id_type=MESH,
        )

    halos = []
    for way in (2, 3, 4, 5, 6, 7, 0, 1):
        for lane in range(4 if ways[way][0] == 0 else 1):
            halos.append((ways[way], len(halos), lane))
    for way, slot, lane in halos:

        @pl.when(there(way))
        def _():
            halo(way, slot, lane).start()

    for at in range(2):
        for lane in range(4):
            pad[at, lane + 1, pl.ds(H, TILE), :] = obj[at, :, pl.ds(lane * H, H)]
    for half in range(2):
        for plane in range(4):
            write_plane(pbuf.at[0, half], plane, probe[half * 2 + plane // 2, plane % 2])
        for chunk in range(CHUNKS):
            pbuf[0, half, 2 * CHUNKS + chunk, pl.ds(16, 8), :] = jnp.zeros((8, R), F32)
    zbuf[...] = jnp.zeros_like(zbuf)
    grad[...] = jnp.zeros_like(grad)

    @pl.loop(0, BATCHES * POS)
    def _(slot):
        high, low = split(jnp.sqrt(patterns[slot]))
        high, low = split(dot(tabs[4], high) + dot(tabs[4], low))
        spat[slot] = dot(high, tabs[5]) + dot(low, tabs[5])

    for way, slot, lane in halos:

        @pl.when(there(way))
        def _():
            halo(way, slot, lane).wait_send()

        @pl.when(there((-way[0], -way[1])))
        def _():
            halo(way, slot, lane).wait_recv()

    lanes = lax.broadcasted_iota(jnp.int32, (R, H), 1)

    def window(slot):
        row = offs[2 * slot] + H
        col = offs[2 * slot + 1] + H
        first = jnp.minimum(col // H, 3)
        return row, first, col - first * H

    def take_patches(batch):
        covered = jnp.zeros((8, R), F32)
        for position in range(POS):
            slot = batch * POS + position
            row, first, shift = window(slot)
            live = slot < cnt[0]
            turn = (H - shift) % H
            for at in range(2):
                turned = [
                    pltpu.roll(pad[at, first + k, pl.ds(row, R), :], turn, 1) for k in range(3)
                ]
                for k in range(2):
                    value = jnp.where(lanes < H - shift, turned[k], turned[k + 1])
                    value = jnp.where(live, value, 0.0)
                    patch[position, at, :, pl.ds(k * H, H)] = value
                    covered = covered + jnp.sum(value * value)
        cover[...] = covered

    take_patches(0)

    def half_planes(ref, mode):
        return read_plane(ref, 2 * mode), read_plane(ref, 2 * mode + 1)

    def run_batch(batch):
        for half in range(2):
            for chunk in range(CHUNKS):
                gbuf[half, 2 * CHUNKS + chunk, pl.ds(16, 8), :] = cover[...]

        @pl.loop(0, 2)
        def _(half):
            for mode in range(2):
                pr, pi = half_planes(pbuf.at[batch, half], mode)
                for position in range(POS):
                    our, oui = patch[position, 0], patch[position, 1]
                    psi = jnp.concatenate([pr * our - pi * oui, pr * oui + pi * our], axis=1)
                    left = left_product((table[0][...], table[1][...]), psi)
                    left = jnp.concatenate([left[:, :R], left[:, R:]], axis=0)
                    both = right_product(left, (table_t[0][...], table_t[1][...]))
                    quads = butterfly(both[:R], both[R:])
                    slot = half * 2 + mode
                    for a in range(2):
                        for b in range(2):
                            for at in range(2):
                                far[position, slot, at, pl.ds(a * HALF, HALF), pl.ds(b * HALF, HALF)] = (
                                    quads[a][b][at]
                                )

        for position in range(POS):

            @pl.loop(0, R // 32)
            def _(tile):
                rows = pl.ds(pl.multiple_of(tile * 32, 32), 32)
                power = jnp.zeros((32, R), F32)
                for mode in range(MODES):
                    re, im = far[position, mode, 0, rows, :], far[position, mode, 1, rows, :]
                    power = power + re * re + im * im
                slot = batch * POS + position
                spat[slot, rows, :] = 1.0 - spat[slot, rows, :] * lax.rsqrt(power + 0.1)

        @pl.loop(0, 2)
        def _(half):
            for mode in range(2):
                pr, pi = half_planes(pbuf.at[batch, half], mode)
                sum_re, sum_im = None, None
                for position in range(POS):
                    slot = half * 2 + mode
                    quads = []
                    for a in range(2):
                        row = []
                        for b in range(2):
                            rows, cols = pl.ds(a * HALF, HALF), pl.ds(b * HALF, HALF)
                            keep = spat[batch * POS + position, rows, cols]
                            row.append(
                                (
                                    far[position, slot, 0, rows, cols] * keep,
                                    far[position, slot, 1, rows, cols] * keep,
                                )
                            )
                        quads.append(row)
                    both = butterfly_transposed(quads)
                    right = right_product(both, (table[0][...], table[1][...]))
                    right = jnp.concatenate([right[:R], right[R:]], axis=1)
                    back = left_product((table_t[0][...], table_t[1][...]), right)
                    dr, di = back[:, :R], back[:, R:]
                    our, oui = patch[position, 0], patch[position, 1]
                    og_re = pr * dr + pi * di
                    og_im = pr * di - pi * dr
                    if mode == 0:

                        @pl.when(half == 0)
                        def _():
                            og[position, 0] = og_re
                            og[position, 1] = og_im

                        @pl.when(half != 0)
                        def _():
                            og[position, 0] += og_re
                            og[position, 1] += og_im
                    else:
                        og[position, 0] += og_re
                        og[position, 1] += og_im
                    pg_re = our * dr + oui * di
                    pg_im = our * di - oui * dr
                    sum_re = pg_re if sum_re is None else sum_re + pg_re
                    sum_im = pg_im if sum_im is None else sum_im + pg_im
                write_plane(gbuf.at[half], 2 * mode, sum_re)
                write_plane(gbuf.at[half], 2 * mode + 1, sum_im)

    def add_gradient(batch):
        rows, firsts = [], []
        for position in range(POS):
            row, first, shift = window(batch * POS + position)
            rows.append(row)
            firsts.append(first)
            turn = shift % H
            for at in range(2):
                low = pltpu.roll(og[position, at, :, pl.ds(0, H)], turn, 1)
                high = pltpu.roll(og[position, at, :, pl.ds(H, H)], turn, 1)
                zbuf[position, at, 1, pl.ds(8, R), :] = jnp.where(lanes >= shift, low, 0.0)
                zbuf[position, at, 2, pl.ds(8, R), :] = jnp.where(lanes >= shift, high, low)
                zbuf[position, at, 3, pl.ds(8, R), :] = jnp.where(lanes >= shift, 0.0, high)

        @pl.loop(0, (TILE + 2 * H) // 16)
        def _(tile):
            base = pl.multiple_of(tile * 16, 16)
            for sub in range(2):
                at_row = base + 8 * sub
                starts = [jnp.clip(at_row - row + 8, 0, R + 8) for row in rows]
                for at in range(2):
                    for lane in range(6):
                        value = grad[at, lane, pl.ds(at_row, 8), :]
                        for position in range(POS):
                            source = jnp.clip(lane - firsts[position] + 1, 0, 4)
                            value = value + zbuf[position, at, source, pl.ds(starts[position], 8), :]
                        grad[at, lane, pl.ds(at_row, 8), :] = value

    def border_copy(index):
        way = ways[index]
        (lane, n_lane), (row, rows) = border(way)
        if way[1] == 0:
            source = grad.at[:, lane, pl.ds(row, rows), :]
            target = hside.at[index]
        elif way[0] == 0:
            source = grad.at[:, pl.ds(lane, n_lane), pl.ds(row, rows), :]
            target = hvert.at[index - 2]
        else:
            source = grad.at[:, lane, pl.ds(row, rows), :]
            target = hcorn.at[index - 4]
        return pltpu.make_async_remote_copy(
            src_ref=source,
            dst_ref=target,
            send_sem=gsend.at[index],
            recv_sem=grecv.at[index],
            device_id=away(way),
            device_id_type=MESH,
        )

    def all_reduce(batch):
        new = pbuf.at[batch + 1]
        old = pbuf.at[batch]

        def copy(source, target, index, to):
            return pltpu.make_async_remote_copy(
                src_ref=source,
                dst_ref=target,
                send_sem=bsend.at[index],
                recv_sem=brecv.at[batch, index],
                device_id=to,
                device_id_type=MESH,
            )

        sent = []

        def send(*args):
            one = copy(*args)
            one.start()
            sent.append(one)

        other = 1 - core
        for part in range(PARTS):
            span = pl.ds(part * CHUNKS, CHUNKS)
            send(gbuf.at[other, span], recv0.at[batch, span], part, sibling)
        for part in range(PARTS):
            span = pl.ds(part * CHUNKS, CHUNKS)
            d1 = ORDER[part][0]
            copy(gbuf.at[other, span], recv0.at[batch, span], part, sibling).wait_recv()
            acc0[span] = gbuf[core, span] + recv0[batch, span]
            for step in STEPS:
                index = 3 + part * 3 + step - 1
                chunk = part * CHUNKS + 4 * ((place[d1] + step) % 4)
                send(acc0.at[pl.ds(chunk, 4)], recv1.at[batch, part, step - 1], index, peer(d1, step))

        take_patches(jnp.minimum(batch + 1, BATCHES - 1))

        for part in range(PARTS):
            d1, d2, _ = ORDER[part]
            own = pl.ds(part * CHUNKS + 4 * place[d1], 4)
            value = acc0[own]
            for step in STEPS:
                index = 3 + part * 3 + step - 1
                copy(acc0.at[own], recv1.at[batch, part, step - 1], index, peer(d1, step)).wait_recv()
                value = value + recv1[batch, part, step - 1]
            acc1[part] = value
            for step in STEPS:
                index = 12 + part * 3 + step - 1
                send(acc1.at[part, (place[d2] + step) % 4], recv2.at[batch, part, step - 1], index, peer(d2, step))

        add_gradient(batch)

        @pl.when(batch == BATCHES - 1)
        def _():
            for index in (2, 3, 4, 5, 6, 7, 0, 1):

                @pl.when(there(ways[index]))
                def _():
                    border_copy(index).start()

        for part in range(PARTS):
            _, d2, d3 = ORDER[part]
            value = acc1[part, place[d2]]
            for step in STEPS:
                index = 12 + part * 3 + step - 1
                copy(acc1.at[part, 0], recv2.at[batch, part, step - 1], index, peer(d2, step)).wait_recv()
                value = value + recv2[batch, part, step - 1]
            cross[batch, part, place[d3]] = value
            for step in STEPS:
                index = 21 + part * 3 + step - 1
                mine = cross.at[batch, part, place[d3]]
                send(mine, mine, index, peer(d3, step))
        sums = []
        for part in range(PARTS):
            d3 = ORDER[part][2]
            for step in STEPS:
                index = 21 + part * 3 + step - 1
                theirs = cross.at[batch, part, (place[d3] + 4 - step) % 4]
                copy(theirs, theirs, index, peer(d3, step)).wait_recv()
            value = cross[batch, part, 0]
            for at in range(1, 4):
                value = value + cross[batch, part, at]
            sums.append(value)
        scale = sums[2][16:] / float(R * R)
        scale = jnp.concatenate([scale, scale, scale], axis=0)
        for part in range(PARTS):
            d1, d2, _ = ORDER[part]
            chunk = part * CHUNKS + 4 * place[d1] + place[d2]
            new[core, chunk] = old[core, chunk] - sums[part] / scale
            for step in STEPS:
                index = 30 + part * 3 + step - 1
                mine = new.at[core, chunk]
                send(mine, mine, index, peer(d2, step))
        for part in range(PARTS):
            d1, d2, _ = ORDER[part]
            for step in STEPS:
                index = 30 + part * 3 + step - 1
                chunk = part * CHUNKS + 4 * place[d1] + (place[d2] + 4 - step) % 4
                theirs = new.at[core, chunk]
                copy(theirs, theirs, index, peer(d2, step)).wait_recv()
            group = new.at[core, pl.ds(part * CHUNKS + 4 * place[d1], 4)]
            for step in STEPS:
                send(group, group, 39 + part * 3 + step - 1, peer(d1, step))
            send(group, group, 48 + part * 4, sibling)
        for step in STEPS:
            for part in range(PARTS):
                d1 = ORDER[part][0]
                group = new.at[core, pl.ds(part * CHUNKS + 4 * ((place[d1] + 4 - step) % 4), 4)]
                copy(group, group, 39 + part * 3 + step - 1, peer(d1, step)).wait_recv()
                send(group, group, 48 + part * 4 + step, sibling)
        for step in range(4):
            for part in range(PARTS):
                d1 = ORDER[part][0]
                group = new.at[other, pl.ds(part * CHUNKS + 4 * ((place[d1] + 4 - step) % 4), 4)]
                copy(group, group, 48 + part * 4 + step, sibling).wait_recv()
        for one in sent:
            one.wait_send()

    @pl.loop(0, BATCHES)
    def _(batch):
        run_batch(batch)
        all_reduce(batch)

    power = jnp.zeros((R, R), F32)
    for half in range(2):
        for plane in range(4):
            value = read_plane(pbuf.at[BATCHES, half], plane)
            probe_out[half * 2 + plane // 2, plane % 2] = value
            power = power + value * value
    top = jnp.max(power)

    for index, way in enumerate(ways):

        @pl.when(there(way))
        def _():
            border_copy(index).wait_send()

        @pl.when(there((-way[0], -way[1])))
        def _():
            border_copy(index).wait_recv()

    def came(lane, row, rows, at):
        value = grad[at, lane + 1, pl.ds(H + row, rows), :]
        if lane == 0:
            value = value + hside[1, at, pl.ds(row, rows), :]
        if lane == 3:
            value = value + hside[0, at, pl.ds(row, rows), :]
        if row == 0:
            value = value + hvert[1, at, lane]
            if lane == 0:
                value = value + hcorn[3, at]
            if lane == 3:
                value = value + hcorn[2, at]
        if row == TILE - H:
            value = value + hvert[0, at, lane]
            if lane == 0:
                value = value + hcorn[1, at]
            if lane == 3:
                value = value + hcorn[0, at]
        return value

    for at in range(2):
        for lane in range(4):
            for row in range(0, TILE, H):
                place_at = (at, pl.ds(row, H), pl.ds(lane * H, H))
                obj_out[place_at] = obj[place_at] - 0.5 * came(lane, row, H, at) / top


def local(object_field, probe, patterns, offsets, counts):
    vmem = pl.BlockSpec(memory_space=pltpu.VMEM)
    smem = pl.BlockSpec(memory_space=pltpu.SMEM)
    dma = pltpu.SemaphoreType.DMA
    return pl.pallas_call(
        whole_kernel,
        out_shape=(
            jax.ShapeDtypeStruct((2, TILE, TILE), F32),
            jax.ShapeDtypeStruct((MODES, 2, R, R), F32),
        ),
        in_specs=[smem, smem, vmem, vmem, vmem, vmem],
        out_specs=(vmem, vmem),
        scratch_shapes=[
            pltpu.VMEM((2, 6, TILE + 2 * H, H), F32),
            pltpu.VMEM((BATCHES + 1, 2, PARTS * CHUNKS, ROWS, R), F32),
            pltpu.VMEM((2, PARTS * CHUNKS, ROWS, R), F32),
            pltpu.VMEM((BATCHES * POS, R, R), F32),
            pltpu.VMEM((POS, 2, R, R), F32),
            pltpu.VMEM((POS, MODES, 2, R, R), F32),
            pltpu.VMEM((POS, 2, R, R), F32),
            pltpu.VMEM((POS, 2, 5, R + 16, H), F32),
            pltpu.VMEM((2, 6, TILE + 2 * H, H), F32),
            pltpu.VMEM((8, R), F32),
            pltpu.VMEM((PARTS * CHUNKS, ROWS, R), F32),
            pltpu.VMEM((PARTS, 4, ROWS, R), F32),
            pltpu.VMEM((BATCHES, PARTS * CHUNKS, ROWS, R), F32),
            pltpu.VMEM((BATCHES, PARTS, 3, 4, ROWS, R), F32),
            pltpu.VMEM((BATCHES, PARTS, 3, ROWS, R), F32),
            pltpu.VMEM((BATCHES, PARTS, 4, ROWS, R), F32),
            pltpu.VMEM((2, 2, TILE, H), F32),
            pltpu.VMEM((2, 2, 4, H, H), F32),
            pltpu.VMEM((4, 2, H, H), F32),
            dma((60,)),
            dma((BATCHES, 60)),
            dma((14,)),
            dma((14,)),
            dma((8,)),
            dma((8,)),
        ],
        compiler_params=pltpu.CompilerParams(
            collective_id=0, has_side_effects=True, vmem_limit_bytes=67043328
        ),
    )(
        offsets.reshape(BATCHES * POS * 2),
        counts.reshape(1),
        object_field,
        probe,
        patterns.reshape(BATCHES * POS, R, R),
        jnp.asarray(tables()),
    )


def solution(mesh):
    placed = (
        P(None, "narrow", "wide"),
        P(),
        P("narrow", "wide", None, None, None),
        P("narrow", "wide", None, None),
        P("narrow", "wide"),
    )
    return jax.shard_map(
        local,
        mesh=mesh,
        in_specs=placed,
        out_specs=(P(None, "narrow", "wide"), P()),
        check_vma=False,
    )
```

time: 810 us -> 184 us (0.23)
  blocking collectives: 280 us -> 0 us
  waiting for transfers between devices: 219 us -> 0 us
  Pallas kernels: 0 us -> 177 us
  starting transfers between devices: 80.5 us -> 0 us
  local copies, waits for them, and re-layouts: 64.4 us -> 5.91 us
  loops' own time: 50.9 us -> 0 us
  other arithmetic: 45.3 us -> 0 us
  matrix products: 30.8 us -> 0 us
  between operations: 31.9 us -> 1.29 us
    psum x3 -> x0, blocking collectives: 280 us -> none  [local(): summed, total_cover = lax.psum((probe_grad, coverage), ('wide', 'narrow'))]
    psum x3 -> x0, waiting for transfers between devices: 202 us -> none  [local(): summed, total_cover = lax.psum((probe_grad, coverage), ('wide', 'narrow'))]
    pallas_call x0 -> x1, Pallas kernels: none -> 177 us  [local(): pl.pallas_call(whole_kernel, out_shape=(jax.ShapeDtypeStruct((2, TILE, TI...]
    ppermute x8 -> x0, starting transfers between devices: 80.4 us -> none  [the longest x4 69.1 us: shifted(): lax.ppermute(value, axis, [(source, source + steps) for source in range(l...]
    another operation x6 -> x0, loops' own time: 50.9 us -> none  [local(): lax.cond(slot_at < count_here, active, inactive, (patch, probe, measured))]
    dynamic_update_slice x6 -> x0, local copies, waits for them, and re-layouts: 38.2 us -> none  [local(): lax.dynamic_update_slice(gradient, old + obj_grad, (zero_at, row_at, col_...]
    dot_general x16 -> x0, matrix products: 30.8 us -> none  [the longest x2 4.5 us: transform(): jnp.einsum('mjk,kl->mjl', left_im, table_im, precision=high)]
    add x8 -> x0, other arithmetic: 19.2 us -> none  [the longest x3 11.6 us: local(): probe_grad = probe_grad + pgrad]
  transfers between devices with their start and end apart: 11 -> 0, of which waited for: 8 -> 0; matrix products, arithmetic and copies ran while one was open for 6% -> 0% of each run, Pallas kernels for 0% -> 0%
where the time goes in v1:
time: 184 us
  Pallas kernels  177 us (96%)
  local copies, waits for them, and re-layouts  5.91 us (3%)
    pallas_call x1, Pallas kernels, local(): pl.pallas_call(whole_kernel, out_shape=(jax.ShapeDtypeStruct((2, TILE, TI...  177 us
    unnamed x5, local copies, waits for them, and re-layouts  5.32 us

profile of v1, /device:TPU:1, one launch (start us, length us, event | category | flops | bytes accessed | tf_op | source)
XLA Modules:
  0.0 184.3 jit_solution(791466130083395800)
XLA Ops:
  1.3 0.8 copy.9
  2.0 0.6 reshape.13.offs
  2.6 177.1 %shard_map.77 = (f32[2,512,512]{2,1,0:T(8,128)}, f32[4,2,256,256]{3,2,1,0:T(8,128)}) custom-call(s32[12]{0:T(128)} %reshape.13.offs, s32[1]{0:T(128)} %bitcast.2.cnt, f32[2,512,512]{2,1,0:T(8,128)} %obj.1, f32[4,2,256,256]{3,2,1,0:T(8,128)} %probe.1, f32[6,256,256]{2,1,0:T(8,128)} %bitcast.3, bf16[6,256,256]{2,1,0:T(8,128)(2,1)} %constant.2.clone.tabs), custom_call_target="tpu_custom_call" | custom-call | tf_op jit(solution)/shard_map/pallas_call | solution.py:597
  179.7 0.0 copy-start
  179.7 3.2 %copy.13 = f32[2,512,512]{2,1,0:T(8,128)} copy(f32[2,512,512]{2,1,0:T(8,128)} %get-tuple-element.4) | data formatting | bytes 4194304
  183.0 0.0 copy-done
  183.0 1.3 copy.14
Async XLA Ops:
  179.7 3.2 %copy-start = (f32[4,2,256,256]{3,2,1,0:T(8,128)S(1)}, f32[4,2,256,256]{3,2,1,0:T(8,128)}, u32[]{:S(2)}) copy-start(f32[4,2,256,256]{3,2,1,0:T(8,128)} %get-tuple-element.5) | copy-start | bytes 6291460

commit v2 on v1

--- a/solution.py
+++ b/solution.py
@@ -156,32 +156,18 @@
 
     sibling = device(place, 1 - core)
 
-    ways = ((-1, 0), (1, 0), (0, -1), (0, 1), (-1, -1), (1, -1), (-1, 1), (1, 1))
+    left, right, above, below = ways = ((-1, 0), (1, 0), (0, -1), (0, 1))
 
     def there(way):
-        dw, dn = way
-        ok = wide >= 0
-        if dw:
-            ok = (wide > 0) if dw < 0 else (wide < n_wide - 1)
-        if dn:
-            ok_n = (x > 0) if dn < 0 else (x < n_narrow - 1)
-            ok = jnp.logical_and(ok, ok_n) if dw else ok_n
-        return ok
+        if way[0]:
+            return (wide > 0) if way[0] < 0 else (wide < n_wide - 1)
+        return (x > 0) if way[1] < 0 else (x < n_narrow - 1)
 
     def away(way):
         return (wide + way[0], x + way[1])
 
-    def border(way):
-        dw, dn = way
-        lane = {-1: (0, 1), 0: (1, 4), 1: (5, 1)}[dw]
-        row = {-1: (0, H), 0: (H, TILE), 1: (H + TILE, H)}[dn]
-        return lane, row
-
-    def edge(way):
-        dw, dn = way
-        lane = {-1: (0, 1), 0: (0, 4), 1: (3, 1)}[dw]
-        row = {-1: (0, H), 0: (0, TILE), 1: (TILE - H, H)}[dn]
-        return lane, row
+    def back(way):
+        return (-way[0], -way[1])
 
     for at in range(2):
         for lane in (0, 5):
@@ -191,7 +177,6 @@
             pad[at, lane, pl.ds(H + TILE, H), :] = jnp.zeros((H, H), F32)
     hside[...] = jnp.zeros_like(hside)
     hvert[...] = jnp.zeros_like(hvert)
-    hcorn[...] = jnp.zeros_like(hcorn)
 
     barrier = pltpu.get_barrier_semaphore()
     pl.semaphore_signal(barrier, inc=1, device_id=sibling, device_id_type=MESH)
@@ -208,27 +193,67 @@
 
     pl.semaphore_wait(barrier, total)
 
-    def halo(way, slot, lane):
-        (lane_to, _), (row_to, rows) = border((-way[0], -way[1]))
-        (lane_from, _), (row_from, _) = edge(way)
+    def neighbour_copy(source, target, send_sem, recv_sem, index, way):
         return pltpu.make_async_remote_copy(
-            src_ref=obj.at[:, pl.ds(row_from, rows), pl.ds((lane_from + lane) * H, H)],
-            dst_ref=pad.at[:, lane_to + lane, pl.ds(row_to, rows), :],
-            send_sem=hsend.at[slot],
-            recv_sem=hrecv.at[slot],
+            src_ref=source,
+            dst_ref=target,
+            send_sem=send_sem.at[index],
+            recv_sem=recv_sem.at[index],
             device_id=away(way),
             device_id_type=MESH,
         )
 
-    halos = []
-    for way in (2, 3, 4, 5, 6, 7, 0, 1):
-        for lane in range(4 if ways[way][0] == 0 else 1):
-            halos.append((ways[way], len(halos), lane))
-    for way, slot, lane in halos:
-
-        @pl.when(there(way))
+    def halo(index):
+        if index < 2:
+            way = ways[index]
+            lane_from, lane_to = ((0, 5), (3, 0))[index]
+            source = obj.at[:, :, pl.ds(lane_from * H, H)]
+            return way, True, neighbour_copy(
+                source, pad.at[:, lane_to, pl.ds(H, TILE), :], hsend, hrecv, index, way
+            )
+        if index < 10:
+            lane = (0, 3, 1, 2)[(index - 2) // 2]
+            side = (index - 2) % 2
+            row_from, row_to = ((0, H + TILE), (TILE - H, 0))[side]
+            source = obj.at[:, pl.ds(row_from, H), pl.ds(lane * H, H)]
+            return ways[2 + side], True, neighbour_copy(
+                source, pad.at[:, lane + 1, pl.ds(row_to, H), :], hsend, hrecv, index, ways[2 + side]
+            )
+        vertical, side = divmod(index - 10, 2)
+        lane_from, lane_to = ((1, 5), (4, 0))[side]
+        rows = pl.ds(vertical * (H + TILE), H)
+        return ways[side], there(ways[2 + vertical]), neighbour_copy(
+            pad.at[:, lane_from, rows, :], pad.at[:, lane_to, rows, :], hsend, hrecv, index, ways[side]
+        )
+
+    def both_there(way, also):
+        return there(way) if also is True else jnp.logical_and(there(way), also)
+
+    def start_if(copy):
+        way, also, one = copy
+
+        @pl.when(both_there(way, also))
         def _():
-            halo(way, slot, lane).start()
+            one.start()
+
+    def wait_send_if(copy):
+        way, also, one = copy
+
+        @pl.when(both_there(way, also))
+        def _():
+            one.wait_send()
+
+    def wait_recv_if(copy):
+        way, also, one = copy
+
+        @pl.when(both_there(back(way), also))
+        def _():
+            one.wait_recv()
+
+    for index in range(2, 10):
+        start_if(halo(index))
+    for index in range(2):
+        start_if(halo(index))
 
     for at in range(2):
         for lane in range(4):
@@ -247,15 +272,14 @@
         high, low = split(dot(tabs[4], high) + dot(tabs[4], low))
         spat[slot] = dot(high, tabs[5]) + dot(low, tabs[5])
 
-    for way, slot, lane in halos:
-
-        @pl.when(there(way))
-        def _():
-            halo(way, slot, lane).wait_send()
-
-        @pl.when(there((-way[0], -way[1])))
-        def _():
-            halo(way, slot, lane).wait_recv()
+    for index in range(2, 6):
+        wait_recv_if(halo(index))
+    for index in range(10, 14):
+        start_if(halo(index))
+    for index in (0, 1, 6, 7, 8, 9, 10, 11, 12, 13):
+        wait_recv_if(halo(index))
+    for index in range(14):
+        wait_send_if(halo(index))
 
     lanes = lax.broadcasted_iota(jnp.int32, (R, H), 1)
 
@@ -294,7 +318,13 @@
                 gbuf[half, 2 * CHUNKS + chunk, pl.ds(16, 8), :] = cover[...]
 
         @pl.loop(0, 2)
-        def _(half):
+        def _(turn):
+            half = (core + turn) % 2
+
+            @pl.when(jnp.logical_and(turn == 1, batch > 0))
+            def _():
+                all_reduce_end(batch - 1)
+
             for mode in range(2):
                 pr, pi = half_planes(pbuf.at[batch, half], mode)
                 for position in range(POS):
@@ -325,7 +355,8 @@
                 spat[slot, rows, :] = 1.0 - spat[slot, rows, :] * lax.rsqrt(power + 0.1)
 
         @pl.loop(0, 2)
-        def _(half):
+        def _(turn):
+            half = (core + 1 + turn) % 2
             for mode in range(2):
                 pr, pi = half_planes(pbuf.at[batch, half], mode)
                 sum_re, sum_im = None, None
@@ -354,12 +385,12 @@
                     og_im = pr * di - pi * dr
                     if mode == 0:
 
-                        @pl.when(half == 0)
+                        @pl.when(turn == 0)
                         def _():
                             og[position, 0] = og_re
                             og[position, 1] = og_im
 
-                        @pl.when(half != 0)
+                        @pl.when(turn != 0)
                         def _():
                             og[position, 0] += og_re
                             og[position, 1] += og_im
@@ -372,6 +403,11 @@
                     sum_im = pg_im if sum_im is None else sum_im + pg_im
                 write_plane(gbuf.at[half], 2 * mode, sum_re)
                 write_plane(gbuf.at[half], 2 * mode + 1, sum_im)
+
+            @pl.when(turn == 0)
+            def _():
+                for part in range(PARTS):
+                    to_sibling(batch, part).start()
 
     def add_gradient(batch):
         rows, firsts = [], []
@@ -402,35 +438,84 @@
                         grad[at, lane, pl.ds(at_row, 8), :] = value
 
     def border_copy(index):
-        way = ways[index]
-        (lane, n_lane), (row, rows) = border(way)
-        if way[1] == 0:
-            source = grad.at[:, lane, pl.ds(row, rows), :]
-            target = hside.at[index]
-        elif way[0] == 0:
-            source = grad.at[:, pl.ds(lane, n_lane), pl.ds(row, rows), :]
-            target = hvert.at[index - 2]
-        else:
-            source = grad.at[:, lane, pl.ds(row, rows), :]
-            target = hcorn.at[index - 4]
+        if index < 4:
+            vertical, side = divmod(index, 2)
+            rows = pl.ds(vertical * (H + TILE), H)
+            return ways[side], True, neighbour_copy(
+                grad.at[:, (0, 5)[side], rows, :], hcorn.at[vertical, side], gsend, grecv, index, ways[side]
+            )
+        if index < 6:
+            side = index - 4
+            return ways[side], True, neighbour_copy(
+                grad.at[:, (0, 5)[side], pl.ds(H, TILE), :], hside.at[side], gsend, grecv, index, ways[side]
+            )
+        lane = (1, 2, 0, 3)[(index - 6) // 2]
+        vertical = (index - 6) % 2
+        rows = pl.ds(vertical * (H + TILE), H)
+        return ways[2 + vertical], True, neighbour_copy(
+            grad.at[:, lane + 1, rows, :], hvert.at[vertical, :, lane], gsend, grecv, index, ways[2 + vertical]
+        )
+
+    def pass_corners():
+        for index in range(4):
+            vertical, side = divmod(index, 2)
+            rows = pl.ds(vertical * (H + TILE), H)
+            lane = (4, 1)[side]
+            way, _, one = border_copy(index)
+
+            @pl.when(there(back(way)))
+            def _():
+                one.wait_recv()
+                for at in range(2):
+                    grad[at, lane, rows, :] += hcorn[vertical, side, at]
+
+        for index in range(10, 14):
+            start_if(border_copy(index))
+
+    def to_sibling(batch, part):
+        span = pl.ds(part * CHUNKS, CHUNKS)
         return pltpu.make_async_remote_copy(
-            src_ref=source,
-            dst_ref=target,
-            send_sem=gsend.at[index],
-            recv_sem=grecv.at[index],
-            device_id=away(way),
+            src_ref=gbuf.at[1 - core, span],
+            dst_ref=recv0.at[batch, span],
+            send_sem=bsend.at[part],
+            recv_sem=brecv.at[batch, part],
+            device_id=sibling,
             device_id_type=MESH,
         )
+
+    def shared(batch, part, step):
+        chunk = part * CHUNKS + 4 * ((place[ORDER[part][0]] + 4 - step) % 4)
+        group = pl.ds(chunk, 4)
+        index = part * 4 + step
+
+        def copy(half):
+            ref = pbuf.at[batch + 1, half, group]
+            return pltpu.make_async_remote_copy(
+                src_ref=ref,
+                dst_ref=ref,
+                send_sem=bsend.at[3 + index],
+                recv_sem=brecv.at[batch, 3 + index],
+                device_id=sibling,
+                device_id_type=MESH,
+            )
+
+        return copy
+
+    def all_reduce_end(batch):
+        for step in range(4):
+            for part in range(PARTS):
+                shared(batch, part, step)(1 - core).wait_recv()
+                shared(batch, part, step)(core).wait_send()
 
     def all_reduce(batch):
         new = pbuf.at[batch + 1]
         old = pbuf.at[batch]
 
-        def copy(source, target, index, to):
+        def copy(source, target, index, to, send=0):
             return pltpu.make_async_remote_copy(
                 src_ref=source,
                 dst_ref=target,
-                send_sem=bsend.at[index],
+                send_sem=bsend.at[send],
                 recv_sem=brecv.at[batch, index],
                 device_id=to,
                 device_id_type=MESH,
@@ -438,105 +523,114 @@
 
         sent = []
 
-        def send(*args):
-            one = copy(*args)
+        def send(source, target, index, to):
+            one = copy(source, target, index, to, 15 + len(sent))
             one.start()
             sent.append(one)
 
-        other = 1 - core
-        for part in range(PARTS):
-            span = pl.ds(part * CHUNKS, CHUNKS)
-            send(gbuf.at[other, span], recv0.at[batch, span], part, sibling)
+        def first_at(part, order):
+            return (place[ORDER[part][1]] + 1 + order) % 4
+
         for part in range(PARTS):
             span = pl.ds(part * CHUNKS, CHUNKS)
             d1 = ORDER[part][0]
-            copy(gbuf.at[other, span], recv0.at[batch, span], part, sibling).wait_recv()
+            to_sibling(batch, part).wait_recv()
             acc0[span] = gbuf[core, span] + recv0[batch, span]
-            for step in STEPS:
-                index = 3 + part * 3 + step - 1
-                chunk = part * CHUNKS + 4 * ((place[d1] + step) % 4)
-                send(acc0.at[pl.ds(chunk, 4)], recv1.at[batch, part, step - 1], index, peer(d1, step))
+            for order in range(4):
+                for step in STEPS:
+                    chunk = part * CHUNKS + 4 * ((place[d1] + step) % 4) + first_at(part, order)
+                    target = recv1.at[batch, part, order, step - 1]
+                    send(acc0.at[chunk], target, 15 + part * 4 + order, peer(d1, step))
 
         take_patches(jnp.minimum(batch + 1, BATCHES - 1))
 
+        lasts = []
+        for order in range(4):
+            for part in range(PARTS):
+                d1, d2, _ = ORDER[part]
+                quarter = recv1.at[batch, part, order]
+                copy(acc0.at[pl.ds(0, 3)], quarter, 15 + part * 4 + order, peer(d1, 1)).wait_recv()
+                value = acc0[part * CHUNKS + 4 * place[d1] + first_at(part, order)]
+                for step in STEPS:
+                    value = value + quarter[step - 1]
+                if order == 3:
+                    lasts.append(value)
+                else:
+                    acc1[part, order] = value
+                    target = recv2.at[batch, part, order]
+                    send(acc1.at[part, order], target, 27 + part, peer(d2, order + 1))
+
         for part in range(PARTS):
-            d1, d2, _ = ORDER[part]
-            own = pl.ds(part * CHUNKS + 4 * place[d1], 4)
-            value = acc0[own]
-            for step in STEPS:
-                index = 3 + part * 3 + step - 1
-                copy(acc0.at[own], recv1.at[batch, part, step - 1], index, peer(d1, step)).wait_recv()
-                value = value + recv1[batch, part, step - 1]
-            acc1[part] = value
-            for step in STEPS:
-                index = 12 + part * 3 + step - 1
-                send(acc1.at[part, (place[d2] + step) % 4], recv2.at[batch, part, step - 1], index, peer(d2, step))
-
+            acc1[part, 3] = lasts[part]
         add_gradient(batch)
 
         @pl.when(batch == BATCHES - 1)
         def _():
-            for index in (2, 3, 4, 5, 6, 7, 0, 1):
-
-                @pl.when(there(ways[index]))
-                def _():
-                    border_copy(index).start()
+            for index in range(10):
+                start_if(border_copy(index))
 
         for part in range(PARTS):
             _, d2, d3 = ORDER[part]
-            value = acc1[part, place[d2]]
+            copy(acc1.at[part, pl.ds(0, 3)], recv2.at[batch, part], 27 + part, peer(d2, 1)).wait_recv()
+            value = acc1[part, 3]
             for step in STEPS:
-                index = 12 + part * 3 + step - 1
-                copy(acc1.at[part, 0], recv2.at[batch, part, step - 1], index, peer(d2, step)).wait_recv()
                 value = value + recv2[batch, part, step - 1]
             cross[batch, part, place[d3]] = value
             for step in STEPS:
-                index = 21 + part * 3 + step - 1
                 mine = cross.at[batch, part, place[d3]]
-                send(mine, mine, index, peer(d3, step))
+                send(mine, mine, 30 + part * 3 + step - 1, peer(d3, step))
+
+        @pl.when(batch == BATCHES - 1)
+        def _():
+            pass_corners()
+
         sums = []
         for part in range(PARTS):
             d3 = ORDER[part][2]
             for step in STEPS:
-                index = 21 + part * 3 + step - 1
                 theirs = cross.at[batch, part, (place[d3] + 4 - step) % 4]
-                copy(theirs, theirs, index, peer(d3, step)).wait_recv()
+                copy(theirs, theirs, 30 + part * 3 + step - 1, peer(d3, step)).wait_recv()
             value = cross[batch, part, 0]
             for at in range(1, 4):
                 value = value + cross[batch, part, at]
             sums.append(value)
         scale = sums[2][16:] / float(R * R)
         scale = jnp.concatenate([scale, scale, scale], axis=0)
+
+        def gather(part, chunk):
+            d1 = ORDER[part][0]
+            ref = new.at[core, chunk]
+            for step in STEPS:
+                send(ref, ref, 48 + part * 3 + step - 1, peer(d1, step))
+
+        chunks = []
         for part in range(PARTS):
             d1, d2, _ = ORDER[part]
             chunk = part * CHUNKS + 4 * place[d1] + place[d2]
+            chunks.append(chunk)
             new[core, chunk] = old[core, chunk] - sums[part] / scale
             for step in STEPS:
-                index = 30 + part * 3 + step - 1
                 mine = new.at[core, chunk]
-                send(mine, mine, index, peer(d2, step))
+                send(mine, mine, 39 + part * 3 + step - 1, peer(d2, step))
         for part in range(PARTS):
-            d1, d2, _ = ORDER[part]
-            for step in STEPS:
-                index = 30 + part * 3 + step - 1
+            gather(part, chunks[part])
+        for step in (1, 3, 2):
+            for part in range(PARTS):
+                d1, d2, _ = ORDER[part]
                 chunk = part * CHUNKS + 4 * place[d1] + (place[d2] + 4 - step) % 4
                 theirs = new.at[core, chunk]
-                copy(theirs, theirs, index, peer(d2, step)).wait_recv()
-            group = new.at[core, pl.ds(part * CHUNKS + 4 * place[d1], 4)]
-            for step in STEPS:
-                send(group, group, 39 + part * 3 + step - 1, peer(d1, step))
-            send(group, group, 48 + part * 4, sibling)
-        for step in STEPS:
+                copy(theirs, theirs, 39 + part * 3 + step - 1, peer(d2, step)).wait_recv()
+                gather(part, chunk)
+        for part in range(PARTS):
+            shared(batch, part, 0)(core).start()
+        for step in (1, 3, 2):
             for part in range(PARTS):
                 d1 = ORDER[part][0]
                 group = new.at[core, pl.ds(part * CHUNKS + 4 * ((place[d1] + 4 - step) % 4), 4)]
-                copy(group, group, 39 + part * 3 + step - 1, peer(d1, step)).wait_recv()
-                send(group, group, 48 + part * 4 + step, sibling)
-        for step in range(4):
-            for part in range(PARTS):
-                d1 = ORDER[part][0]
-                group = new.at[other, pl.ds(part * CHUNKS + 4 * ((place[d1] + 4 - step) % 4), 4)]
-                copy(group, group, 48 + part * 4 + step, sibling).wait_recv()
+                copy(group, group, 48 + part * 3 + step - 1, peer(d1, step)).wait_recv()
+                shared(batch, part, step)(core).start()
+        for part in range(PARTS):
+            to_sibling(batch, part).wait_send()
         for one in sent:
             one.wait_send()
 
@@ -544,6 +638,8 @@
     def _(batch):
         run_batch(batch)
         all_reduce(batch)
+
+    all_reduce_end(BATCHES - 1)
 
     power = jnp.zeros((R, R), F32)
     for half in range(2):
@@ -553,15 +649,10 @@
             power = power + value * value
     top = jnp.max(power)
 
-    for index, way in enumerate(ways):
-
-        @pl.when(there(way))
-        def _():
-            border_copy(index).wait_send()
-
-        @pl.when(there((-way[0], -way[1])))
-        def _():
-            border_copy(index).wait_recv()
+    for index in range(4, 14):
+        wait_recv_if(border_copy(index))
+    for index in range(14):
+        wait_send_if(border_copy(index))
 
     def came(lane, row, rows, at):
         value = grad[at, lane + 1, pl.ds(H + row, rows), :]
@@ -571,16 +662,8 @@
             value = value + hside[0, at, pl.ds(row, rows), :]
         if row == 0:
             value = value + hvert[1, at, lane]
-            if lane == 0:
-                value = value + hcorn[3, at]
-            if lane == 3:
-                value = value + hcorn[2, at]
         if row == TILE - H:
             value = value + hvert[0, at, lane]
-            if lane == 0:
-                value = value + hcorn[1, at]
-            if lane == 3:
-                value = value + hcorn[0, at]
         return value
 
     for at in range(2):
@@ -616,18 +699,18 @@
             pltpu.VMEM((PARTS * CHUNKS, ROWS, R), F32),
             pltpu.VMEM((PARTS, 4, ROWS, R), F32),
             pltpu.VMEM((BATCHES, PARTS * CHUNKS, ROWS, R), F32),
-            pltpu.VMEM((BATCHES, PARTS, 3, 4, ROWS, R), F32),
+            pltpu.VMEM((BATCHES, PARTS, 4, 3, ROWS, R), F32),
             pltpu.VMEM((BATCHES, PARTS, 3, ROWS, R), F32),
             pltpu.VMEM((BATCHES, PARTS, 4, ROWS, R), F32),
             pltpu.VMEM((2, 2, TILE, H), F32),
             pltpu.VMEM((2, 2, 4, H, H), F32),
-            pltpu.VMEM((4, 2, H, H), F32),
-            dma((60,)),
-            dma((BATCHES, 60)),
+            pltpu.VMEM((2, 2, 2, H, H), F32),
+            dma((114,)),
+            dma((BATCHES, 57)),
             dma((14,)),
             dma((14,)),
-            dma((8,)),
-            dma((8,)),
+            dma((14,)),
+            dma((14,)),
         ],
         compiler_params=pltpu.CompilerParams(
             collective_id=0, has_side_effects=True, vmem_limit_bytes=67043328

time: 184 us -> 156 us (0.85)
  Pallas kernels: 177 us -> 148 us
    pallas_call x1, Pallas kernels: 177 us -> 148 us  [local(): pl.pallas_call(whole_kernel, out_shape=(jax.ShapeDtypeStruct((2, TILE, TI...]
where the time goes in v2:
time: 156 us
  Pallas kernels  148 us (95%)
  local copies, waits for them, and re-layouts  5.91 us (4%)
    pallas_call x1, Pallas kernels, local(): pl.pallas_call(whole_kernel, out_shape=(jax.ShapeDtypeStruct((2, TILE, TI...  148 us
    unnamed x5, local copies, waits for them, and re-layouts  5.32 us

profile of v2, /device:TPU:1, one launch (start us, length us, event | category | flops | bytes accessed | tf_op | source)
XLA Modules:
  0.0 155.7 jit_solution(10907482157298853611)
XLA Ops:
  1.3 0.8 copy.9
  2.0 0.6 reshape.13.offs
  2.6 148.5 %shard_map.77 = (f32[2,512,512]{2,1,0:T(8,128)}, f32[4,2,256,256]{3,2,1,0:T(8,128)}) custom-call(s32[12]{0:T(128)} %reshape.13.offs, s32[1]{0:T(128)} %bitcast.2.cnt, f32[2,512,512]{2,1,0:T(8,128)} %obj.1, f32[4,2,256,256]{3,2,1,0:T(8,128)} %probe.1, f32[6,256,256]{2,1,0:T(8,128)} %bitcast.3, bf16[6,256,256]{2,1,0:T(8,128)(2,1)} %constant.2.clone.tabs), custom_call_target="tpu_custom_call" | custom-call | tf_op jit(solution)/shard_map/pallas_call | solution.py:680
  151.1 0.0 copy-start
  151.1 3.2 %copy.13 = f32[2,512,512]{2,1,0:T(8,128)} copy(f32[2,512,512]{2,1,0:T(8,128)} %get-tuple-element.4) | data formatting | bytes 4194304
  154.4 0.0 copy-done
  154.4 1.3 copy.14
Async XLA Ops:
  151.1 3.2 %copy-start = (f32[4,2,256,256]{3,2,1,0:T(8,128)S(1)}, f32[4,2,256,256]{3,2,1,0:T(8,128)}, u32[]{:S(2)}) copy-start(f32[4,2,256,256]{3,2,1,0:T(8,128)} %get-tuple-element.5) | copy-start | bytes 6291460

commit v3 on v2

--- a/solution.py
+++ b/solution.py
@@ -22,7 +22,7 @@
 CHUNKS = 16
 ROWS = 24
 ORDER = ((0, 1, 2), (1, 2, 0), (2, 0, 1))
-STEPS = (1, 2, 3)
+STEPS = (2, 1, 3)
 
 
 def tables():
@@ -129,11 +129,11 @@
 
 
 def whole_kernel(
-    offs, cnt, obj, probe, patterns, tabs,
+    offs, cnt, obj, probe_in, patterns_in, tabs_in,
     obj_out, probe_out,
-    pad, pbuf, gbuf, spat, patch, far, og, zbuf, grad, cover,
+    probe, tabs, pad, pbuf, gbuf, spat, patch, far, og, zbuf, grad, cover,
     acc0, acc1, recv0, recv1, recv2, cross, hside, hvert, hcorn,
-    bsend, brecv, hsend, hrecv, gsend, grecv,
+    load, bsend, brecv, hsend, hrecv, gsend, grecv,
 ):
     wide = lax.axis_index("wide")
     x = lax.axis_index("narrow")
@@ -169,14 +169,14 @@
     def back(way):
         return (-way[0], -way[1])
 
-    for at in range(2):
-        for lane in (0, 5):
-            pad[at, lane] = jnp.zeros((TILE + 2 * H, H), F32)
-        for lane in range(1, 5):
-            pad[at, lane, pl.ds(0, H), :] = jnp.zeros((H, H), F32)
-            pad[at, lane, pl.ds(H + TILE, H), :] = jnp.zeros((H, H), F32)
-    hside[...] = jnp.zeros_like(hside)
-    hvert[...] = jnp.zeros_like(hvert)
+    loads = [
+        pltpu.make_async_copy(source, target, load.at[index])
+        for index, (source, target) in enumerate(
+            ((tabs_in, tabs), (patterns_in, spat), (probe_in, probe))
+        )
+    ]
+    for one in loads:
+        one.start()
 
     barrier = pltpu.get_barrier_semaphore()
     pl.semaphore_signal(barrier, inc=1, device_id=sibling, device_id_type=MESH)
@@ -255,9 +255,36 @@
     for index in range(2):
         start_if(halo(index))
 
+    for side in range(2):
+        lane = (0, 5)[side]
+
+        @pl.when(jnp.logical_not(there(ways[side])))
+        def _():
+            for at in range(2):
+                pad[at, lane, pl.ds(H, TILE), :] = jnp.zeros((TILE, H), F32)
+            hside[1 - side] = jnp.zeros((2, TILE, H), F32)
+
+        for vertical in range(2):
+
+            @pl.when(jnp.logical_not(jnp.logical_and(there(ways[side]), there(ways[2 + vertical]))))
+            def _():
+                for at in range(2):
+                    pad[at, lane, pl.ds(vertical * (H + TILE), H), :] = jnp.zeros((H, H), F32)
+
+    for vertical in range(2):
+
+        @pl.when(jnp.logical_not(there(ways[2 + vertical])))
+        def _():
+            for at in range(2):
+                for lane in range(1, 5):
+                    pad[at, lane, pl.ds(vertical * (H + TILE), H), :] = jnp.zeros((H, H), F32)
+            hvert[1 - vertical] = jnp.zeros((2, 4, H, H), F32)
+
     for at in range(2):
         for lane in range(4):
             pad[at, lane + 1, pl.ds(H, TILE), :] = obj[at, :, pl.ds(lane * H, H)]
+    for one in loads:
+        one.wait()
     for half in range(2):
         for plane in range(4):
             write_plane(pbuf.at[0, half], plane, probe[half * 2 + plane // 2, plane % 2])
@@ -268,7 +295,7 @@
 
     @pl.loop(0, BATCHES * POS)
     def _(slot):
-        high, low = split(jnp.sqrt(patterns[slot]))
+        high, low = split(jnp.sqrt(spat[slot]))
         high, low = split(dot(tabs[4], high) + dot(tabs[4], low))
         spat[slot] = dot(high, tabs[5]) + dot(low, tabs[5])
 
@@ -284,8 +311,8 @@
     lanes = lax.broadcasted_iota(jnp.int32, (R, H), 1)
 
     def window(slot):
-        row = offs[2 * slot] + H
-        col = offs[2 * slot + 1] + H
+        row = offs[0, slot] + H
+        col = offs[1, slot] + H
         first = jnp.minimum(col // H, 3)
         return row, first, col - first * H
 
@@ -357,6 +384,7 @@
         @pl.loop(0, 2)
         def _(turn):
             half = (core + 1 + turn) % 2
+            grads = [[jnp.where(turn == 0, 0.0, og[p, at]) for at in range(2)] for p in range(POS)]
             for mode in range(2):
                 pr, pi = half_planes(pbuf.at[batch, half], mode)
                 sum_re, sum_im = None, None
@@ -383,26 +411,17 @@
                     our, oui = patch[position, 0], patch[position, 1]
                     og_re = pr * dr + pi * di
                     og_im = pr * di - pi * dr
-                    if mode == 0:
-
-                        @pl.when(turn == 0)
-                        def _():
-                            og[position, 0] = og_re
-                            og[position, 1] = og_im
-
-                        @pl.when(turn != 0)
-                        def _():
-                            og[position, 0] += og_re
-                            og[position, 1] += og_im
-                    else:
-                        og[position, 0] += og_re
-                        og[position, 1] += og_im
+                    grads[position][0] += og_re
+                    grads[position][1] += og_im
                     pg_re = our * dr + oui * di
                     pg_im = our * di - oui * dr
                     sum_re = pg_re if sum_re is None else sum_re + pg_re
                     sum_im = pg_im if sum_im is None else sum_im + pg_im
                 write_plane(gbuf.at[half], 2 * mode, sum_re)
                 write_plane(gbuf.at[half], 2 * mode + 1, sum_im)
+            for p in range(POS):
+                for at in range(2):
+                    og[p, at] = grads[p][at]
 
             @pl.when(turn == 0)
             def _():
@@ -444,13 +463,15 @@
             return ways[side], True, neighbour_copy(
                 grad.at[:, (0, 5)[side], rows, :], hcorn.at[vertical, side], gsend, grecv, index, ways[side]
             )
-        if index < 6:
-            side = index - 4
+        if index < 12:
+            piece, side = divmod(index - 4, 2)
             return ways[side], True, neighbour_copy(
-                grad.at[:, (0, 5)[side], pl.ds(H, TILE), :], hside.at[side], gsend, grecv, index, ways[side]
+                grad.at[:, (0, 5)[side], pl.ds(H + H * piece, H), :],
+                hside.at[side, :, pl.ds(H * piece, H), :],
+                gsend, grecv, index, ways[side],
             )
-        lane = (1, 2, 0, 3)[(index - 6) // 2]
-        vertical = (index - 6) % 2
+        lane = (1, 2, 0, 3)[(index - 12) // 2]
+        vertical = (index - 12) % 2
         rows = pl.ds(vertical * (H + TILE), H)
         return ways[2 + vertical], True, neighbour_copy(
             grad.at[:, lane + 1, rows, :], hvert.at[vertical, :, lane], gsend, grecv, index, ways[2 + vertical]
@@ -469,8 +490,16 @@
                 for at in range(2):
                     grad[at, lane, rows, :] += hcorn[vertical, side, at]
 
-        for index in range(10, 14):
-            start_if(border_copy(index))
+    def border_turn(batch, turn):
+        @pl.when(batch == BATCHES - 1)
+        def _():
+            if turn == 0:
+                for index in range(4):
+                    start_if(border_copy(index))
+            if turn == 2:
+                pass_corners()
+            for index in (2 * turn + 12, 2 * turn + 13, 2 * turn + 4, 2 * turn + 5):
+                start_if(border_copy(index))
 
     def to_sibling(batch, part):
         span = pl.ds(part * CHUNKS, CHUNKS)
@@ -542,7 +571,8 @@
                     target = recv1.at[batch, part, order, step - 1]
                     send(acc0.at[chunk], target, 15 + part * 4 + order, peer(d1, step))
 
-        take_patches(jnp.minimum(batch + 1, BATCHES - 1))
+        add_gradient(batch)
+        border_turn(batch, 0)
 
         lasts = []
         for order in range(4):
@@ -562,12 +592,11 @@
 
         for part in range(PARTS):
             acc1[part, 3] = lasts[part]
-        add_gradient(batch)
-
-        @pl.when(batch == BATCHES - 1)
+        border_turn(batch, 1)
+
+        @pl.when(batch < BATCHES - 1)
         def _():
-            for index in range(10):
-                start_if(border_copy(index))
+            take_patches(batch + 1)
 
         for part in range(PARTS):
             _, d2, d3 = ORDER[part]
@@ -580,10 +609,7 @@
                 mine = cross.at[batch, part, place[d3]]
                 send(mine, mine, 30 + part * 3 + step - 1, peer(d3, step))
 
-        @pl.when(batch == BATCHES - 1)
-        def _():
-            pass_corners()
-
+        border_turn(batch, 2)
         sums = []
         for part in range(PARTS):
             d3 = ORDER[part][2]
@@ -614,6 +640,7 @@
                 send(mine, mine, 39 + part * 3 + step - 1, peer(d2, step))
         for part in range(PARTS):
             gather(part, chunks[part])
+        border_turn(batch, 3)
         for step in (1, 3, 2):
             for part in range(PARTS):
                 d1, d2, _ = ORDER[part]
@@ -649,9 +676,9 @@
             power = power + value * value
     top = jnp.max(power)
 
-    for index in range(4, 14):
+    for index in range(4, 20):
         wait_recv_if(border_copy(index))
-    for index in range(14):
+    for index in range(20):
         wait_send_if(border_copy(index))
 
     def came(lane, row, rows, at):
@@ -675,17 +702,20 @@
 
 def local(object_field, probe, patterns, offsets, counts):
     vmem = pl.BlockSpec(memory_space=pltpu.VMEM)
+    hbm = pl.BlockSpec(memory_space=pltpu.HBM)
     smem = pl.BlockSpec(memory_space=pltpu.SMEM)
     dma = pltpu.SemaphoreType.DMA
     return pl.pallas_call(
         whole_kernel,
         out_shape=(
-            jax.ShapeDtypeStruct((2, TILE, TILE), F32),
-            jax.ShapeDtypeStruct((MODES, 2, R, R), F32),
+            pltpu.VMEM((2, TILE, TILE), F32),
+            pltpu.VMEM((MODES, 2, R, R), F32),
         ),
-        in_specs=[smem, smem, vmem, vmem, vmem, vmem],
+        in_specs=[smem, smem, vmem, hbm, hbm, hbm],
         out_specs=(vmem, vmem),
         scratch_shapes=[
+            pltpu.VMEM((MODES, 2, R, R), F32),
+            pltpu.VMEM((6, R, R), BF16),
             pltpu.VMEM((2, 6, TILE + 2 * H, H), F32),
             pltpu.VMEM((BATCHES + 1, 2, PARTS * CHUNKS, ROWS, R), F32),
             pltpu.VMEM((2, PARTS * CHUNKS, ROWS, R), F32),
@@ -705,18 +735,19 @@
             pltpu.VMEM((2, 2, TILE, H), F32),
             pltpu.VMEM((2, 2, 4, H, H), F32),
             pltpu.VMEM((2, 2, 2, H, H), F32),
+            dma((3,)),
             dma((114,)),
             dma((BATCHES, 57)),
             dma((14,)),
             dma((14,)),
-            dma((14,)),
-            dma((14,)),
+            dma((20,)),
+            dma((20,)),
         ],
         compiler_params=pltpu.CompilerParams(
-            collective_id=0, has_side_effects=True, vmem_limit_bytes=67043328
+            collective_id=0, has_side_effects=True, vmem_limit_bytes=56 * 1024 * 1024
         ),
     )(
-        offsets.reshape(BATCHES * POS * 2),
+        offsets.reshape(BATCHES * POS, 2).T,
         counts.reshape(1),
         object_field,
         probe,

time: 156 us -> 138 us (0.88)
  Pallas kernels: 148 us -> 134 us
  local copies, waits for them, and re-layouts: 5.91 us -> 2.64 us
    pallas_call x1, Pallas kernels: 148 us -> 134 us  [local(): pl.pallas_call(whole_kernel, out_shape=(pltpu.VMEM((2, TILE, TILE), F32),...]
    unnamed x5 -> x2, local copies, waits for them, and re-layouts: 5.32 us -> 2.64 us
where the time goes in v3:
time: 138 us
  Pallas kernels  134 us (97%)
  local copies, waits for them, and re-layouts  2.64 us (2%)
    pallas_call x1, Pallas kernels, local(): pl.pallas_call(whole_kernel, out_shape=(pltpu.VMEM((2, TILE, TILE), F32),...  134 us

profile of v3, /device:TPU:1, one launch (start us, length us, event | category | flops | bytes accessed | tf_op | source)
XLA Modules:
  0.0 137.9 jit_solution(13549834248602395046)
XLA Ops:
  1.3 134.0 %shard_map.77 = (f32[2,512,512]{2,1,0:T(8,128)S(1)}, f32[4,2,256,256]{3,2,1,0:T(8,128)S(1)}) custom-call(s32[2,6]{1,0:T(2,128)} %bitcast.7, s32[1]{0:T(128)} %bitcast.5.cnt, f32[2,512,512]{2,1,0:T(8,128)} %obj.1, f32[4,2,256,256]{3,2,1,0:T(8,128)} %probe_in.1, f32[6,256,256]{2,1,0:T(8,128)} %bitcast.6, bf16[6,256,256]{2,1,0:T(8,128)(2,1)} %constant.2.clone.tabs_in), custom_call_target="tpu_custom_call" | custom-call | tf_op jit(solution)/shard_map/pallas_call | solution.py:708
  135.3 1.3 copy.10
  136.6 1.3 copy.11

commit v4 on v3

--- a/solution.py
+++ b/solution.py
@@ -129,9 +129,9 @@
 
 
 def whole_kernel(
-    offs, cnt, obj, probe_in, patterns_in, tabs_in,
+    offs, cnt, obj_in, probe_in, patterns_in, tabs_in,
     obj_out, probe_out,
-    probe, tabs, pad, pbuf, gbuf, spat, patch, far, og, zbuf, grad, cover,
+    obj, probe, tabs, pad, pbuf, gbuf, spat, patch, far, og, zbuf, grad, cover,
     acc0, acc1, recv0, recv1, recv2, cross, hside, hvert, hcorn,
     load, bsend, brecv, hsend, hrecv, gsend, grecv,
 ):
@@ -172,7 +172,7 @@
     loads = [
         pltpu.make_async_copy(source, target, load.at[index])
         for index, (source, target) in enumerate(
-            ((tabs_in, tabs), (patterns_in, spat), (probe_in, probe))
+            ((obj_in, obj), (tabs_in, tabs), (patterns_in, spat), (probe_in, probe))
         )
     ]
     for one in loads:
@@ -192,6 +192,7 @@
             pl.semaphore_signal(barrier, inc=1, device_id=away(way), device_id_type=MESH)
 
     pl.semaphore_wait(barrier, total)
+    loads[0].wait()
 
     def neighbour_copy(source, target, send_sem, recv_sem, index, way):
         return pltpu.make_async_remote_copy(
@@ -283,7 +284,7 @@
     for at in range(2):
         for lane in range(4):
             pad[at, lane + 1, pl.ds(H, TILE), :] = obj[at, :, pl.ds(lane * H, H)]
-    for one in loads:
+    for one in loads[1:]:
         one.wait()
     for half in range(2):
         for plane in range(4):
@@ -370,10 +371,8 @@
                                 )
 
         for position in range(POS):
-
-            @pl.loop(0, R // 32)
-            def _(tile):
-                rows = pl.ds(pl.multiple_of(tile * 32, 32), 32)
+            for tile in range(R // 32):
+                rows = pl.ds(tile * 32, 32)
                 power = jnp.zeros((32, R), F32)
                 for mode in range(MODES):
                     re, im = far[position, mode, 0, rows, :], far[position, mode, 1, rows, :]
@@ -381,10 +380,8 @@
                 slot = batch * POS + position
                 spat[slot, rows, :] = 1.0 - spat[slot, rows, :] * lax.rsqrt(power + 0.1)
 
-        @pl.loop(0, 2)
-        def _(turn):
+        for turn in range(2):
             half = (core + 1 + turn) % 2
-            grads = [[jnp.where(turn == 0, 0.0, og[p, at]) for at in range(2)] for p in range(POS)]
             for mode in range(2):
                 pr, pi = half_planes(pbuf.at[batch, half], mode)
                 sum_re, sum_im = None, None
@@ -411,20 +408,19 @@
                     our, oui = patch[position, 0], patch[position, 1]
                     og_re = pr * dr + pi * di
                     og_im = pr * di - pi * dr
-                    grads[position][0] += og_re
-                    grads[position][1] += og_im
+                    if turn == 0 and mode == 0:
+                        og[position, 0] = og_re
+                        og[position, 1] = og_im
+                    else:
+                        og[position, 0] += og_re
+                        og[position, 1] += og_im
                     pg_re = our * dr + oui * di
                     pg_im = our * di - oui * dr
                     sum_re = pg_re if sum_re is None else sum_re + pg_re
                     sum_im = pg_im if sum_im is None else sum_im + pg_im
                 write_plane(gbuf.at[half], 2 * mode, sum_re)
                 write_plane(gbuf.at[half], 2 * mode + 1, sum_im)
-            for p in range(POS):
-                for at in range(2):
-                    og[p, at] = grads[p][at]
-
-            @pl.when(turn == 0)
-            def _():
+            if turn == 0:
                 for part in range(PARTS):
                     to_sibling(batch, part).start()
 
@@ -674,7 +670,7 @@
             value = read_plane(pbuf.at[BATCHES, half], plane)
             probe_out[half * 2 + plane // 2, plane % 2] = value
             power = power + value * value
-    top = jnp.max(power)
+    part_of_top = 0.5 / jnp.max(power)
 
     for index in range(4, 20):
         wait_recv_if(border_copy(index))
@@ -697,7 +693,18 @@
         for lane in range(4):
             for row in range(0, TILE, H):
                 place_at = (at, pl.ds(row, H), pl.ds(lane * H, H))
-                obj_out[place_at] = obj[place_at] - 0.5 * came(lane, row, H, at) / top
+                obj_out[place_at] = obj[place_at] - came(lane, row, H, at) * part_of_top
+
+
+def ship_kernel(obj, probe, obj_out, probe_out, sems):
+    copies = [
+        pltpu.make_async_copy(obj, obj_out, sems.at[0]),
+        pltpu.make_async_copy(probe, probe_out, sems.at[1]),
+    ]
+    for one in copies:
+        one.start()
+    for one in copies:
+        one.wait()
 
 
 def local(object_field, probe, patterns, offsets, counts):
@@ -705,15 +712,16 @@
     hbm = pl.BlockSpec(memory_space=pltpu.HBM)
     smem = pl.BlockSpec(memory_space=pltpu.SMEM)
     dma = pltpu.SemaphoreType.DMA
-    return pl.pallas_call(
+    done = pl.pallas_call(
         whole_kernel,
         out_shape=(
             pltpu.VMEM((2, TILE, TILE), F32),
             pltpu.VMEM((MODES, 2, R, R), F32),
         ),
-        in_specs=[smem, smem, vmem, hbm, hbm, hbm],
+        in_specs=[smem, smem, hbm, hbm, hbm, hbm],
         out_specs=(vmem, vmem),
         scratch_shapes=[
+            pltpu.VMEM((2, TILE, TILE), F32),
             pltpu.VMEM((MODES, 2, R, R), F32),
             pltpu.VMEM((6, R, R), BF16),
             pltpu.VMEM((2, 6, TILE + 2 * H, H), F32),
@@ -735,7 +743,7 @@
             pltpu.VMEM((2, 2, TILE, H), F32),
             pltpu.VMEM((2, 2, 4, H, H), F32),
             pltpu.VMEM((2, 2, 2, H, H), F32),
-            dma((3,)),
+            dma((4,)),
             dma((114,)),
             dma((BATCHES, 57)),
             dma((14,)),
@@ -754,6 +762,17 @@
         patterns.reshape(BATCHES * POS, R, R),
         jnp.asarray(tables()),
     )
+    return pl.pallas_call(
+        ship_kernel,
+        out_shape=(
+            jax.ShapeDtypeStruct((2, TILE, TILE), F32),
+            jax.ShapeDtypeStruct((MODES, 2, R, R), F32),
+        ),
+        in_specs=[vmem, vmem],
+        out_specs=(hbm, hbm),
+        scratch_shapes=[dma((2,))],
+        compiler_params=pltpu.CompilerParams(vmem_limit_bytes=1024 * 1024),
+    )(*done)
 
 
 def solution(mesh):

time: 138 us -> 135 us (0.978)
  local copies, waits for them, and re-layouts: 2.64 us -> 0 us
    unnamed x2 -> x0, local copies, waits for them, and re-layouts: 2.64 us -> none
    pallas_call x1, Pallas kernels: 134 us -> 132 us  [local(): pl.pallas_call(whole_kernel, out_shape=(pltpu.VMEM((2, TILE, TILE), F32),...]
    pallas_call x0 -> x1, Pallas kernels: none -> 2.03 us  [local(): pl.pallas_call(ship_kernel, out_shape=(jax.ShapeDtypeStruct((2, TILE, TIL...]
where the time goes in v4:
time: 135 us
  Pallas kernels  134 us (99%)
    pallas_call x1, Pallas kernels, local(): pl.pallas_call(whole_kernel, out_shape=(pltpu.VMEM((2, TILE, TILE), F32),...  132 us

profile of v4, /device:TPU:1, one launch (start us, length us, event | category | flops | bytes accessed | tf_op | source)
XLA Modules:
  0.0 135.3 jit_solution(16098541352458255265)
XLA Ops:
  1.3 132.0 %shard_map.77 = (f32[2,512,512]{2,1,0:T(8,128)S(1)}, f32[4,2,256,256]{3,2,1,0:T(8,128)S(1)}) custom-call(s32[2,6]{1,0:T(2,128)} %bitcast.7, s32[1]{0:T(128)} %bitcast.5.cnt, f32[2,512,512]{2,1,0:T(8,128)} %obj_in.1, f32[4,2,256,256]{3,2,1,0:T(8,128)} %probe_in.1, f32[6,256,256]{2,1,0:T(8,128)} %bitcast.6, bf16[6,256,256]{2,1,0:T(8,128)(2,1)} %constant.2.clone.tabs_in), custom_call_target="tpu_custom_call" | custom-call | tf_op jit(solution)/shard_map/pallas_call | solution.py:715
  133.2 2.0 %shard_map.78 = (f32[2,512,512]{2,1,0:T(8,128)}, f32[4,2,256,256]{3,2,1,0:T(8,128)}) custom-call(f32[2,512,512]{2,1,0:T(8,128)S(1)} %get-tuple-element.4.obj, f32[4,2,256,256]{3,2,1,0:T(8,128)S(1)} %get-tuple-element.5.probe), custom_call_target="tpu_custom_call" | custom-call | tf_op jit(solution)/shard_map/pallas_call | solution.py:765

commit v5 on v4

--- a/solution.py
+++ b/solution.py
@@ -21,7 +21,8 @@
 PARTS = 3
 CHUNKS = 16
 ROWS = 24
-ORDER = ((0, 1, 2), (1, 2, 0), (2, 0, 1))
+ORDER = ((1, 2, 0), (2, 0, 1), (0, 1, 2))
+KEPT = (24, 24, 16)
 STEPS = (2, 1, 3)
 
 
@@ -438,19 +439,31 @@
                 zbuf[position, at, 2, pl.ds(8, R), :] = jnp.where(lanes >= shift, high, low)
                 zbuf[position, at, 3, pl.ds(8, R), :] = jnp.where(lanes >= shift, 0.0, high)
 
-        @pl.loop(0, (TILE + 2 * H) // 16)
-        def _(tile):
-            base = pl.multiple_of(tile * 16, 16)
+        def add_rows(base, which):
             for sub in range(2):
-                at_row = base + 8 * sub
+                at_row = pl.multiple_of(base + 8 * sub, 8)
                 starts = [jnp.clip(at_row - row + 8, 0, R + 8) for row in rows]
                 for at in range(2):
-                    for lane in range(6):
+                    for lane in which:
                         value = grad[at, lane, pl.ds(at_row, 8), :]
                         for position in range(POS):
                             source = jnp.clip(lane - firsts[position] + 1, 0, 4)
                             value = value + zbuf[position, at, source, pl.ds(starts[position], 8), :]
                         grad[at, lane, pl.ds(at_row, 8), :] = value
+
+        @pl.loop(0, 2 * H // 16)
+        def _(tile):
+            add_rows(tile * 16 + (tile // (H // 16)) * TILE, range(6))
+
+        @pl.loop(0, TILE // 16)
+        def _(tile):
+            add_rows(H + tile * 16, (0, 5))
+
+        border_turn(batch, 0)
+
+        @pl.loop(0, TILE // 16)
+        def _(tile):
+            add_rows(H + tile * 16, range(1, 5))
 
     def border_copy(index):
         if index < 4:
@@ -514,7 +527,7 @@
         index = part * 4 + step
 
         def copy(half):
-            ref = pbuf.at[batch + 1, half, group]
+            ref = pbuf.at[batch + 1, half, group, pl.ds(0, KEPT[part])]
             return pltpu.make_async_remote_copy(
                 src_ref=ref,
                 dst_ref=ref,
@@ -531,6 +544,19 @@
             for part in range(PARTS):
                 shared(batch, part, step)(1 - core).wait_recv()
                 shared(batch, part, step)(core).wait_send()
+
+    def gather_sent(batch):
+        for index in range(45):
+            part = (index // 3) % 3
+            ref = pbuf.at[batch + 1, core, part, pl.ds(0, KEPT[part])]
+            pltpu.make_async_remote_copy(
+                src_ref=ref,
+                dst_ref=ref,
+                send_sem=bsend.at[15 + 54 + index],
+                recv_sem=brecv.at[batch, 0],
+                device_id=sibling,
+                device_id_type=MESH,
+            ).wait_send()
 
     def all_reduce(batch):
         new = pbuf.at[batch + 1]
@@ -560,6 +586,7 @@
             span = pl.ds(part * CHUNKS, CHUNKS)
             d1 = ORDER[part][0]
             to_sibling(batch, part).wait_recv()
+            to_sibling(batch, part).wait_send()
             acc0[span] = gbuf[core, span] + recv0[batch, span]
             for order in range(4):
                 for step in STEPS:
@@ -568,7 +595,10 @@
                     send(acc0.at[chunk], target, 15 + part * 4 + order, peer(d1, step))
 
         add_gradient(batch)
-        border_turn(batch, 0)
+
+        @pl.when(batch > 0)
+        def _():
+            gather_sent(batch - 1)
 
         lasts = []
         for order in range(4):
@@ -606,6 +636,8 @@
                 send(mine, mine, 30 + part * 3 + step - 1, peer(d3, step))
 
         border_turn(batch, 2)
+        for one in sent[:45]:
+            one.wait_send()
         sums = []
         for part in range(PARTS):
             d3 = ORDER[part][2]
@@ -621,7 +653,7 @@
 
         def gather(part, chunk):
             d1 = ORDER[part][0]
-            ref = new.at[core, chunk]
+            ref = new.at[core, chunk, pl.ds(0, KEPT[part])]
             for step in STEPS:
                 send(ref, ref, 48 + part * 3 + step - 1, peer(d1, step))
 
@@ -632,7 +664,7 @@
             chunks.append(chunk)
             new[core, chunk] = old[core, chunk] - sums[part] / scale
             for step in STEPS:
-                mine = new.at[core, chunk]
+                mine = new.at[core, chunk, pl.ds(0, KEPT[part])]
                 send(mine, mine, 39 + part * 3 + step - 1, peer(d2, step))
         for part in range(PARTS):
             gather(part, chunks[part])
@@ -641,7 +673,7 @@
             for part in range(PARTS):
                 d1, d2, _ = ORDER[part]
                 chunk = part * CHUNKS + 4 * place[d1] + (place[d2] + 4 - step) % 4
-                theirs = new.at[core, chunk]
+                theirs = new.at[core, chunk, pl.ds(0, KEPT[part])]
                 copy(theirs, theirs, 39 + part * 3 + step - 1, peer(d2, step)).wait_recv()
                 gather(part, chunk)
         for part in range(PARTS):
@@ -649,12 +681,12 @@
         for step in (1, 3, 2):
             for part in range(PARTS):
                 d1 = ORDER[part][0]
-                group = new.at[core, pl.ds(part * CHUNKS + 4 * ((place[d1] + 4 - step) % 4), 4)]
+                group = new.at[
+                    core, pl.ds(part * CHUNKS + 4 * ((place[d1] + 4 - step) % 4), 4), pl.ds(0, KEPT[part])
+                ]
                 copy(group, group, 48 + part * 3 + step - 1, peer(d1, step)).wait_recv()
                 shared(batch, part, step)(core).start()
-        for part in range(PARTS):
-            to_sibling(batch, part).wait_send()
-        for one in sent:
+        for one in sent[45:54]:
             one.wait_send()
 
     @pl.loop(0, BATCHES)
@@ -662,6 +694,7 @@
         run_batch(batch)
         all_reduce(batch)
 
+    gather_sent(BATCHES - 1)
     all_reduce_end(BATCHES - 1)
 
     power = jnp.zeros((R, R), F32)

time: 135 us -> 134 us (level)
  Pallas kernels: 134 us -> 132 us
    pallas_call x1, Pallas kernels: 132 us -> 130 us  [local(): pl.pallas_call(whole_kernel, out_shape=(pltpu.VMEM((2, TILE, TILE), F32),...]
where the time goes in v5:
time: 134 us
  Pallas kernels  132 us (99%)
    pallas_call x1, Pallas kernels, local(): pl.pallas_call(whole_kernel, out_shape=(pltpu.VMEM((2, TILE, TILE), F32),...  130 us

profile of v5, /device:TPU:1, one launch (start us, length us, event | category | flops | bytes accessed | tf_op | source)
XLA Modules:
  0.0 133.7 jit_solution(639904573424164936)
XLA Ops:
  1.3 130.4 %shard_map.77 = (f32[2,512,512]{2,1,0:T(8,128)S(1)}, f32[4,2,256,256]{3,2,1,0:T(8,128)S(1)}) custom-call(s32[2,6]{1,0:T(2,128)} %bitcast.7, s32[1]{0:T(128)} %bitcast.5.cnt, f32[2,512,512]{2,1,0:T(8,128)} %obj_in.1, f32[4,2,256,256]{3,2,1,0:T(8,128)} %probe_in.1, f32[6,256,256]{2,1,0:T(8,128)} %bitcast.6, bf16[6,256,256]{2,1,0:T(8,128)(2,1)} %constant.2.clone.tabs_in), custom_call_target="tpu_custom_call" | custom-call | tf_op jit(solution)/shard_map/pallas_call | solution.py:748
  131.7 2.0 %shard_map.78 = (f32[2,512,512]{2,1,0:T(8,128)}, f32[4,2,256,256]{3,2,1,0:T(8,128)}) custom-call(f32[2,512,512]{2,1,0:T(8,128)S(1)} %get-tuple-element.4.obj, f32[4,2,256,256]{3,2,1,0:T(8,128)S(1)} %get-tuple-element.5.probe), custom_call_target="tpu_custom_call" | custom-call | tf_op jit(solution)/shard_map/pallas_call | solution.py:798

commit v6 on v5

--- a/solution.py
+++ b/solution.py
@@ -694,11 +694,12 @@
         run_batch(batch)
         all_reduce(batch)
 
-    gather_sent(BATCHES - 1)
-    all_reduce_end(BATCHES - 1)
-
     power = jnp.zeros((R, R), F32)
-    for half in range(2):
+    for turn in range(2):
+        half = (core + turn) % 2
+        if turn == 1:
+            gather_sent(BATCHES - 1)
+            all_reduce_end(BATCHES - 1)
         for plane in range(4):
             value = read_plane(pbuf.at[BATCHES, half], plane)
             probe_out[half * 2 + plane // 2, plane % 2] = value

time: 134 us -> 134 us (level)
  no operation moved by 1% of the time
where the time goes in v6:
time: 134 us
  Pallas kernels  133 us (99%)
    pallas_call x1, Pallas kernels, local(): pl.pallas_call(whole_kernel, out_shape=(pltpu.VMEM((2, TILE, TILE), F32),...  131 us

profile of v6, /device:TPU:1, one launch (start us, length us, event | category | flops | bytes accessed | tf_op | source)
XLA Modules:
  0.0 134.0 jit_solution(10409723167832976848)
XLA Ops:
  1.3 130.7 %shard_map.77 = (f32[2,512,512]{2,1,0:T(8,128)S(1)}, f32[4,2,256,256]{3,2,1,0:T(8,128)S(1)}) custom-call(s32[2,6]{1,0:T(2,128)} %bitcast.7, s32[1]{0:T(128)} %bitcast.5.cnt, f32[2,512,512]{2,1,0:T(8,128)} %obj_in.1, f32[4,2,256,256]{3,2,1,0:T(8,128)} %probe_in.1, f32[6,256,256]{2,1,0:T(8,128)} %bitcast.6, bf16[6,256,256]{2,1,0:T(8,128)(2,1)} %constant.2.clone.tabs_in), custom_call_target="tpu_custom_call" | custom-call | tf_op jit(solution)/shard_map/pallas_call | solution.py:749
  132.0 2.0 %shard_map.78 = (f32[2,512,512]{2,1,0:T(8,128)}, f32[4,2,256,256]{3,2,1,0:T(8,128)}) custom-call(f32[2,512,512]{2,1,0:T(8,128)S(1)} %get-tuple-element.4.obj, f32[4,2,256,256]{3,2,1,0:T(8,128)S(1)} %get-tuple-element.5.probe), custom_call_target="tpu_custom_call" | custom-call | tf_op jit(solution)/shard_map/pallas_call | solution.py:799
